TPU v7x, 32 devices: a whole 2x2x4 slice. The times are simulated.
32 devices in a mesh: sub: 8 (over z, y), dom: 4 (over x, core).
Axes of the slice: x: 2, y: 2, z: 4, core: 2. Of those that a mesh axis runs over, the one named last changes fastest.
Arguments:
- source_points: float32 [128, 3, 4096], P(('sub', 'dom')), may hold values from -4 to 4
- boundary: float32 [128, 8, 6, 128], P(('sub', 'dom')), may hold values from -4 to 4, as said below
- poses: float32 [12, 128], replicated, may hold values from -2 to 2, as said below
- anchor: float32 [128], P(('sub', 'dom')), may hold values from 0.3 to 3
- edge_target: int32 [128, 4], P(('sub', 'dom')), may hold values from 0 to 47, as said below
- corr_tile: int32 [128, 4, 4], P(('sub', 'dom')), may hold values from 0 to 7
- corr_source: int32 [128, 4, 4, 128], P(('sub', 'dom')), may hold values from 0 to 4095
- corr_lane: int32 [128, 4, 4, 128], P(('sub', 'dom')), may hold values from 0 to 127
Outputs:
- refined_pose: float32 [12, 128], P(None, ('sub', 'dom'))
Inputs may be any that keep to these rules, and one draw needn't show every extreme that they name: `poses`: each column holds a rotation matrix, row-major, followed by a translation. `boundary`: in every column of 6 entries the last 3 form a unit vector. `edge_target`: entry v of scan s names scan v % 16 of the previous (v // 16 = 0), the same (1) or the next (2) submap along the closed chain of submaps; it never names s itself; one scan may be named by several edges of s.
All inputs are finite; a program needn't handle non-finite values.
Results may differ from a plain program's by a relative error of at most 0.0001.
Values sent between devices are 32-bit elements; how exact they have to be, the bound alone decides.
No kernel may reach another device: no remote copies, remote signals or barrier semaphores. Data moves between devices by JAX's collectives and lax.ppermute only.
A program may use at most 64 MiB of HBM per device.

v0:
```python
import jax
import jax.numpy as jnp
from jax import lax
from jax.sharding import PartitionSpec as P

CG_ITERS = 2
GN_ITERS = 2


FINEST = lax.Precision.HIGHEST


def from_behind(block, axis, distance):
    devices = range(lax.axis_size(axis))
    route = [((i - distance) % len(devices), i) for i in devices]
    return lax.ppermute(block, axis, route)


def cayley(vector):
    first, second, third = (vector[0], vector[1], vector[2])
    length_sq = first * first + second * second + third * third
    inverse = 1.0 / (1.0 + length_sq)
    trace_part = 1.0 - length_sq
    entries = [
        [
            trace_part + 2.0 * first * first,
            2.0 * first * second - 2.0 * third,
            2.0 * first * third + 2.0 * second,
        ],
        [
            2.0 * first * second + 2.0 * third,
            trace_part + 2.0 * second * second,
            2.0 * second * third - 2.0 * first,
        ],
        [
            2.0 * first * third - 2.0 * second,
            2.0 * second * third + 2.0 * first,
            trace_part + 2.0 * third * third,
        ],
    ]
    return jnp.stack([jnp.stack(line) for line in entries]) * inverse


def rotate(matrix, vector):
    return jnp.stack(
        [
            matrix[row_id, 0] * vector[0]
            + matrix[row_id, 1] * vector[1]
            + matrix[row_id, 2] * vector[2]
            for row_id in range(3)
        ]
    )


def update(pose, increment):
    rotation = pose[:9].reshape(3, 3, -1)
    turn_mat = cayley(0.5 * increment[:3])
    rotated = jnp.stack(
        [
            jnp.stack(
                [
                    turn_mat[row_id, 0] * rotation[0, col_id]
                    + turn_mat[row_id, 1] * rotation[1, col_id]
                    + turn_mat[row_id, 2] * rotation[2, col_id]
                    for col_id in range(3)
                ]
            )
            for row_id in range(3)
        ]
    )
    moved_to = rotate(turn_mat, pose[9:]) + increment[3:]
    return jnp.concatenate([rotated.reshape(9, -1), moved_to], axis=0)


def scan_terms(points, pose_here, target_tiles, target_pose, sources, lane_ids):
    edge_count = sources.shape[0]
    picked = jnp.take(points, sources, axis=1)
    placed = rotate(pose_here[:9].reshape(3, 3), picked) + pose_here[9:, None, None, None]
    spread_lanes = jnp.broadcast_to(lane_ids[:, :, None, :], target_tiles.shape)
    chosen = jnp.take_along_axis(target_tiles, spread_lanes, axis=3)
    rotation = target_pose[:9].reshape(3, 3, edge_count)[:, :, :, None, None]
    shifted = target_pose[9:, :, None, None]
    target = (
        rotate(rotation, jnp.stack([chosen[:, :, 0], chosen[:, :, 1], chosen[:, :, 2]])) + shifted
    )
    normal = rotate(rotation, jnp.stack([chosen[:, :, 3], chosen[:, :, 4], chosen[:, :, 5]]))
    offset = target - placed
    misfit = normal[0] * offset[0] + normal[1] * offset[1] + normal[2] * offset[2]
    turned = jnp.stack(
        [
            placed[1] * normal[2] - placed[2] * normal[1],
            placed[2] * normal[0] - placed[0] * normal[2],
            placed[0] * normal[1] - placed[1] * normal[0],
        ]
    )
    jacobian = jnp.concatenate([turned, normal], axis=0).reshape(6, edge_count, -1)
    samples = jacobian.shape[2]
    blocks = jnp.einsum("aem,bem->eab", jacobian, jacobian, precision=FINEST) / samples
    slopes = (
        jnp.einsum("aem,em->ea", jacobian, misfit.reshape(edge_count, -1), precision=FINEST)
        / samples
    )
    return (blocks, slopes)


def window_order(sub_index, groups, scan_sub):
    slot_ids = (sub_index + jnp.arange(3, dtype=jnp.int32) - 1) % groups
    return (slot_ids[:, None] * scan_sub + jnp.arange(scan_sub, dtype=jnp.int32)[None, :]).reshape(
        -1
    )


def global_sum(value):
    return lax.psum(value, ("sub", "dom"))


def spread_out(own_part):
    pieces = [from_behind(own_part, "sub", offset_by) for offset_by in (1, -1)]
    before, middle, beyond = (
        lax.all_gather(pieces[0], "dom", axis=1, tiled=True),
        lax.all_gather(own_part, "dom", axis=1, tiled=True),
        lax.all_gather(pieces[1], "dom", axis=1, tiled=True),
    )
    nearby = jnp.concatenate([before, middle, beyond], axis=1)
    return nearby


def collect(partial_value):
    layers = partial_value.shape[0]
    scan_sub = partial_value.shape[2] // 3
    shared = lax.psum_scatter(
        partial_value.reshape(layers, 6, 3, scan_sub), "dom", scatter_dimension=3, tiled=True
    )
    summed = shared[:, :, 1]
    for slot_id, offset_by in ((0, -1), (2, 1)):
        summed = summed + from_behind(shared[:, :, slot_id], "sub", offset_by)
    return summed


def local(source_points, boundary, poses, anchor, edge_target, corr_tile, corr_source, corr_lane):
    scan_dev = source_points.shape[0]
    edge_count = edge_target.shape[1]
    groups = lax.axis_size("sub")
    scan_sub = scan_dev * lax.axis_size("dom")
    sub_index = lax.axis_index("sub")
    dom_index = lax.axis_index("dom")
    window_index = window_order(sub_index, groups, scan_sub)
    middle = lax.all_gather(boundary, "dom", axis=0, tiled=True)
    pieces = [from_behind(middle, "sub", offset_by) for offset_by in (1, -1)]
    window_tiles = jnp.concatenate([pieces[0], middle, pieces[1]], axis=0)
    window_pose = jnp.take(poses, window_index, axis=1)
    own_start = scan_sub + dom_index * scan_dev
    source_at = (own_start + jnp.arange(scan_dev, dtype=jnp.int32))[:, None] + jnp.zeros(
        (1, edge_count), jnp.int32
    )
    from_end = source_at.reshape(-1)
    to_end = edge_target.reshape(-1)
    win_width = 3 * scan_sub
    for turn_id in range(GN_ITERS):
        own_pose = lax.dynamic_slice_in_dim(window_pose, own_start, scan_dev, 1)

        def per_scan(per_item, window_pose=window_pose):
            points, pose_here, targets, tile_ids, sources, lane_ids = per_item
            return scan_terms(
                points,
                pose_here,
                window_tiles[targets[:, None], tile_ids],
                jnp.take(window_pose, targets, axis=1),
                sources,
                lane_ids,
            )

        blocks, slopes = lax.map(
            per_scan, (source_points, own_pose.T, edge_target, corr_tile, corr_source, corr_lane)
        )
        blocks = blocks.reshape(-1, 6, 6)
        slopes = slopes.reshape(-1, 6)
        diag_terms = jnp.diagonal(blocks, axis1=1, axis2=2)
        empty = jnp.zeros((6, win_width), jnp.float32)
        right_part = empty.at[:, from_end].add(slopes.T).at[:, to_end].add(-slopes.T)
        diag_part = empty.at[:, from_end].add(diag_terms.T).at[:, to_end].add(diag_terms.T)
        totals = collect(jnp.stack([right_part, diag_part]))
        right_side = totals[0]
        diagonal_sum = totals[1] + anchor[None, :]

        def apply_system(vector, blocks=blocks):
            nearby = spread_out(vector)
            spread = nearby[:, from_end] - nearby[:, to_end]
            pushed = jnp.einsum("kab,bk->ak", blocks, spread, precision=FINEST)
            partial_value = (
                jnp.zeros((6, win_width), jnp.float32)
                .at[:, from_end]
                .add(pushed)
                .at[:, to_end]
                .add(-pushed)
            )
            return collect(partial_value[None])[0] + anchor[None, :] * vector

        residual = right_side
        scaled = residual / diagonal_sum
        direction = scaled
        energy = global_sum(jnp.sum(residual * scaled))
        increment = jnp.zeros((6, scan_dev), jnp.float32)
        for sweep in range(CG_ITERS):
            image = apply_system(direction)
            step_len = energy / global_sum(jnp.sum(direction * image))
            increment = increment + step_len * direction
            residual = residual - step_len * image
            if sweep + 1 < CG_ITERS:
                scaled = residual / diagonal_sum
                renewed = global_sum(jnp.sum(residual * scaled))
                direction = scaled + renewed / energy * direction
                energy = renewed
        window_pose = update(window_pose, spread_out(increment))
    return lax.dynamic_slice_in_dim(window_pose, own_start, scan_dev, 1)


def solution(mesh):
    in_specs = (
        P(("sub", "dom"), None, None),
        P(("sub", "dom"), None, None, None),
        P(),
        P(("sub", "dom")),
        P(("sub", "dom"), None),
        P(("sub", "dom"), None, None),
        P(("sub", "dom"), None, None, None),
        P(("sub", "dom"), None, None, None),
    )
    out_specs = P(None, ("sub", "dom"))
    return jax.shard_map(local, mesh=mesh, in_specs=in_specs, out_specs=out_specs, check_vma=False)
```

profile of v0, /device:TPU:1, one launch (start us, length us, event | category | flops | bytes accessed | tf_op | source)
XLA Modules:
  0.0 1411.8 jit_solution(11835580075408723627)
XLA Ops:
  0.0 8.1 all_gather.57
  14.5 5.6 copy.252
  29.7 440.6 %while.24 = (s32[]{:T(128)}, f32[4,4,6,6]{3,1,0,2:T(4,128)S(1)}, f32[4,4,6]{2,1,0:T(4,128)S(1)}, f32[4,12]{1,0:T(4,128)S(1)}, f32[4,3,4096]{1,2,0:T(8,128)}, /*i...) while((s32[]{:T(128)}, f32[4,4,6,6]{3,1,0,2:T(4,128)S(1)}, ...), condition=%wide.region_1.5_spmd, body=%wide.region_0.0_spmd.sunk | while | flops 1492314 | bytes 1967897 | solution.py:173
  31.5 5.5 gather_fusion.3
  38.1 5.4 multiply_add_fusion.60
  45.8 91.5 %gather_fusion.1 = f32[12288]{0:T(1024)S(1)} fusion(f32[4,4,6,128]{3,2,1,0:T(8,128)S(1)} %bitcast.1328, s32[12288]{0:T(1024)S(1)} %reshape.2974), kind=kCustom, calls=%fused_computation.2.clone.clone.1 | custom fusion | bytes 294912 | tf_op jit(solution)/shard_map/while/body/eval_jaxpr/jit(take_along_axis)/gather | solution.py:80
  141.6 5.5 gather_fusion.3
  148.3 5.4 multiply_add_fusion.60
  155.9 91.5 %gather_fusion.1 = f32[12288]{0:T(1024)S(1)} fusion(f32[4,4,6,128]{3,2,1,0:T(8,128)S(1)} %bitcast.1328, s32[12288]{0:T(1024)S(1)} %reshape.2974), kind=kCustom, calls=%fused_computation.2.clone.clone.1 | custom fusion | bytes 294912 | tf_op jit(solution)/shard_map/while/body/eval_jaxpr/jit(take_along_axis)/gather | solution.py:80
  251.8 5.5 gather_fusion.3
  258.4 5.4 multiply_add_fusion.60
  266.1 91.5 %gather_fusion.1 = f32[12288]{0:T(1024)S(1)} fusion(f32[4,4,6,128]{3,2,1,0:T(8,128)S(1)} %bitcast.1328, s32[12288]{0:T(1024)S(1)} %reshape.2974), kind=kCustom, calls=%fused_computation.2.clone.clone.1 | custom fusion | bytes 294912 | tf_op jit(solution)/shard_map/while/body/eval_jaxpr/jit(take_along_axis)/gather | solution.py:80
  361.9 5.5 gather_fusion.3
  368.6 5.4 multiply_add_fusion.60
  376.2 91.5 %gather_fusion.1 = f32[12288]{0:T(1024)S(1)} fusion(f32[4,4,6,128]{3,2,1,0:T(8,128)S(1)} %bitcast.1328, s32[12288]{0:T(1024)S(1)} %reshape.2974), kind=kCustom, calls=%fused_computation.2.clone.clone.1 | custom fusion | bytes 294912 | tf_op jit(solution)/shard_map/while/body/eval_jaxpr/jit(take_along_axis)/gather | solution.py:80
  473.8 11.0 all-reduce
  494.7 8.0 all-gather.1
  515.9 10.2 all-reduce.1
  534.5 38.2 %all-reduce.7 = (f32[]{:T(128)}, f32[]{:T(128)}) all-reduce(f32[]{:T(128)} %get-tuple-element.259, f32[]{:T(128)} %get-tuple-element.258), channel_id=1, replica_groups=mesh['sub'=8,'dom'=4] {'sub','dom'}, use_global_device_ids=true, to_apply=%region_8.12 | all-reduce | flops 2 | bytes 16 | tf_op jit(solution)/shard_map/psum | solution.py:114
  574.7 42.3 %psum.58 = f32[]{:T(128)} all-reduce(f32[]{:T(128)} %get-tuple-element.341), channel_id=1, replica_groups=mesh['sub'=8,'dom'=4] {'sub','dom'}, use_global_device_ids=true, to_apply=%region_15.19 | all-reduce | flops 1 | bytes 8 | tf_op jit(solution)/shard_map/psum | solution.py:114
  622.4 7.1 all-gather.4
  629.5 5.5 all-gather.3
  643.0 10.2 all-reduce.2
  659.1 38.5 %psum.59 = f32[]{:T(128)} all-reduce(f32[]{:T(128)} %fusion.120), channel_id=1, replica_groups=mesh['sub'=8,'dom'=4] {'sub','dom'}, use_global_device_ids=true, to_apply=%region_20.24 | all-reduce | flops 1 | bytes 8 | tf_op jit(solution)/shard_map/psum | solution.py:114
  703.0 7.2 all-gather.7
  710.2 5.5 all-gather.6
  721.9 440.6 %while.25 = (s32[]{:T(128)}, f32[4,4,6,6]{3,1,0,2:T(4,128)S(1)}, f32[4,4,6]{2,1,0:T(4,128)S(1)}, f32[4,12]{1,0:T(4,128)S(1)}, f32[4,3,4096]{1,2,0:T(8,128)}, /*i...) while((s32[]{:T(128)}, f32[4,4,6,6]{3,1,0,2:T(4,128)S(1)}, ...), condition=%wide.region_22.26_spmd, body=%wide.region_21.25_spmd.sunk | while | flops 1492314 | bytes 1967897 | solution.py:173
  723.7 5.5 gather_fusion.7
  738.0 91.5 %gather_fusion.5 = f32[12288]{0:T(1024)S(1)} fusion(f32[4,4,6,128]{3,2,1,0:T(8,128)S(1)} %bitcast.1329, s32[12288]{0:T(1024)S(1)} %reshape.2987), kind=kCustom, calls=%fused_computation.6.clone.clone.1 | custom fusion | bytes 294912 | tf_op jit(solution)/shard_map/while/body/eval_jaxpr/jit(take_along_axis)/gather | solution.py:80
  833.8 5.5 gather_fusion.7
  848.1 91.5 %gather_fusion.5 = f32[12288]{0:T(1024)S(1)} fusion(f32[4,4,6,128]{3,2,1,0:T(8,128)S(1)} %bitcast.1329, s32[12288]{0:T(1024)S(1)} %reshape.2987), kind=kCustom, calls=%fused_computation.6.clone.clone.1 | custom fusion | bytes 294912 | tf_op jit(solution)/shard_map/while/body/eval_jaxpr/jit(take_along_axis)/gather | solution.py:80
  944.0 5.5 gather_fusion.7
  950.6 5.4 multiply_add_fusion.62
  958.3 91.5 %gather_fusion.5 = f32[12288]{0:T(1024)S(1)} fusion(f32[4,4,6,128]{3,2,1,0:T(8,128)S(1)} %bitcast.1329, s32[12288]{0:T(1024)S(1)} %reshape.2987), kind=kCustom, calls=%fused_computation.6.clone.clone.1 | custom fusion | bytes 294912 | tf_op jit(solution)/shard_map/while/body/eval_jaxpr/jit(take_along_axis)/gather | solution.py:80
  1054.1 5.5 gather_fusion.7
  1060.7 5.4 multiply_add_fusion.62
  1068.4 91.5 %gather_fusion.5 = f32[12288]{0:T(1024)S(1)} fusion(f32[4,4,6,128]{3,2,1,0:T(8,128)S(1)} %bitcast.1329, s32[12288]{0:T(1024)S(1)} %reshape.2987), kind=kCustom, calls=%fused_computation.6.clone.clone.1 | custom fusion | bytes 294912 | tf_op jit(solution)/shard_map/while/body/eval_jaxpr/jit(take_along_axis)/gather | solution.py:80
  1166.0 10.5 all-reduce.3
  1186.6 8.0 all-gather.10
  1207.8 10.2 all-reduce.4
  1224.0 38.2 %all-reduce.6 = (f32[]{:T(128)}, f32[]{:T(128)}) all-reduce(f32[]{:T(128)} %get-tuple-element.257, f32[]{:T(128)} %get-tuple-element.256), channel_id=1, replica_groups=mesh['sub'=8,'dom'=4] {'sub','dom'}, use_global_device_ids=true, to_apply=%region_29.33 | all-reduce | flops 2 | bytes 16 | tf_op jit(solution)/shard_map/psum | solution.py:114
  1264.1 42.0 %psum.62 = f32[]{:T(128)} all-reduce(f32[]{:T(128)} %get-tuple-element.336), channel_id=1, replica_groups=mesh['sub'=8,'dom'=4] {'sub','dom'}, use_global_device_ids=true, to_apply=%region_36.40 | all-reduce | flops 1 | bytes 8 | tf_op jit(solution)/shard_map/psum | solution.py:114
  1311.6 7.2 all-gather.13
  1318.7 5.5 all-gather.12
  1332.2 10.2 all-reduce.5
  1348.4 38.7 %psum.63 = f32[]{:T(128)} all-reduce(f32[]{:T(128)} %fusion.113), channel_id=1, replica_groups=mesh['sub'=8,'dom'=4] {'sub','dom'}, use_global_device_ids=true, to_apply=%region_41.45 | all-reduce | flops 1 | bytes 8 | tf_op jit(solution)/shard_map/psum | solution.py:114
  1392.7 7.1 all-gather.16
  1399.9 5.5 all-gather.15
  (549 shorter events, 212.5 us)
Async XLA Ops:
  0.0 20.4 %copy-start.5 = (u32[32]{0:T(128)S(1)}, u32[32]{0:T(128)}, u32[]{:S(2)}) copy-start(u32[32]{0:T(128)} %constant.294) | copy-start | bytes 388
  0.0 20.3 %copy-start.4 = (s32[4,4]{1,0:T(4,128)S(1)}, s32[4,4]{1,0:T(4,128)}, u32[]{:S(2)}) copy-start(s32[4,4]{1,0:T(4,128)} %param.22) | copy-start | bytes 196
  8.1 18.0 %collective-permute-start = (f32[16,8,6,128]{3,1,2,0:T(8,128)S(1)}, f32[16,8,6,128]{3,1,2,0:T(8,128)S(1)}, u32[]{:S(2)}, u32[]{:S(2)}) collective-permute-start(f32[16,8,6,128]{3,1,2,0:T(8,128)S(1)} %all_gather.57), channel_id=1, source_target_pairs={{28,0},{0,4},{4,8},{8,12},{12,16},{16,20},{20,24},{24,28},{29,1},{... | collective-permute-start | bytes 1179656 | tf_op jit(solution)/shard_map/ppermute | solution.py:16
  9.4 18.7 %collective-permute-start.1 = (f32[16,8,6,128]{3,1,2,0:T(8,128)S(1)}, f32[16,8,6,128]{3,1,2,0:T(8,128)S(1)}, u32[]{:S(2)}, u32[]{:S(2)}) collective-permute-start(f32[16,8,6,128]{3,1,2,0:T(8,128)S(1)} %all_gather.57), channel_id=1, source_target_pairs={{4,0},{8,4},{12,8},{16,12},{20,16},{24,20},{28,24},{0,28},{5,1},{9... | collective-permute-start | bytes 1179656 | tf_op jit(solution)/shard_map/ppermute | solution.py:16
  14.5 15.2 %copy-start = (s32[4,4,4,128]{3,2,1,0:T(4,128)S(1)}, s32[4,4,4,128]{3,2,1,0:T(4,128)}, u32[]{:S(2)}) copy-start(s32[4,4,4,128]{3,2,1,0:T(4,128)} %param.24) | copy-start | bytes 98308
  14.5 15.2 %copy-start.1 = (s32[4,4,4,128]{3,2,1,0:T(4,128)S(1)}, s32[4,4,4,128]{3,2,1,0:T(4,128)}, u32[]{:S(2)}) copy-start(s32[4,4,4,128]{3,2,1,0:T(4,128)} %param.25) | copy-start | bytes 98308
  14.5 15.2 %copy-start.3 = (s32[4,4,4]{2,1,0:T(4,128)S(1)}, s32[4,4,4]{2,1,0:T(4,128)}, u32[]{:S(2)}) copy-start(s32[4,4,4]{2,1,0:T(4,128)} %param.23) | copy-start | bytes 772
  29.7 463.4 %copy-start.2 = (f32[4]{0:T(128)S(1)}, f32[4]{0:T(128)}, u32[]{:S(2)}) copy-start(f32[4]{0:T(128)} %param.21) | copy-start | bytes 52
  484.9 3.8 collective-permute-start.2
  487.9 5.2 collective-permute-start.3
  493.2 9.6 collective-permute-start.5
  493.2 14.8 %collective-permute-start.4 = (f32[6,4]{0,1:T(4,128)S(1)}, f32[6,4]{0,1:T(4,128)S(1)}, u32[]{:S(2)}, u32[]{:S(2)}) collective-permute-start(f32[6,4]{0,1:T(4,128)S(1)} %fusion.130), channel_id=1, source_target_pairs={{28,0},{0,4},{4,8},{8,12},{12,16},{16,20},{20,24},{24,28},{29,1},{... | collective-permute-start | bytes 296 | tf_op jit(solution)/shard_map/ppermute | solution.py:16
  526.1 3.3 collective-permute-start.6
  528.6 5.1 collective-permute-start.7
  618.2 11.3 collective-permute-start.8
  619.7 15.4 %collective-permute-start.9 = (f32[6,4]{0,1:T(4,128)S(1)}, f32[6,4]{0,1:T(4,128)S(1)}, u32[]{:S(2)}, u32[]{:S(2)}) collective-permute-start(f32[6,4]{0,1:T(4,128)S(1)} %multiply_add_fusion.21), channel_id=1, source_target_pairs={{4,0},{8,4},{12,8},{16,12},{20,16},{24,20},{28,24},{0,28},{5,1},{9... | collective-permute-start | bytes 296 | tf_op jit(solution)/shard_map/ppermute | solution.py:16
  653.2 2.5 collective-permute-start.10
  653.3 5.2 collective-permute-start.11
  698.8 11.4 collective-permute-start.12
  699.8 16.0 %collective-permute-start.13 = (f32[6,4]{0,1:T(4,128)S(1)}, f32[6,4]{0,1:T(4,128)S(1)}, u32[]{:S(2)}, u32[]{:S(2)}) collective-permute-start(f32[6,4]{0,1:T(4,128)S(1)} %multiply_add_fusion.20), channel_id=1, source_target_pairs={{4,0},{8,4},{12,8},{16,12},{20,16},{24,20},{28,24},{0,28},{5,1},{9... | collective-permute-start | bytes 296 | tf_op jit(solution)/shard_map/ppermute | solution.py:16
  1176.5 2.5 collective-permute-start.14
  1177.1 5.2 collective-permute-start.15
  1182.4 12.3 collective-permute-start.16
  1182.4 17.5 %collective-permute-start.17 = (f32[6,4]{0,1:T(4,128)S(1)}, f32[6,4]{0,1:T(4,128)S(1)}, u32[]{:S(2)}, u32[]{:S(2)}) collective-permute-start(f32[6,4]{0,1:T(4,128)S(1)} %fusion.132), channel_id=1, source_target_pairs={{4,0},{8,4},{12,8},{16,12},{20,16},{24,20},{28,24},{0,28},{5,1},{9... | collective-permute-start | bytes 296 | tf_op jit(solution)/shard_map/ppermute | solution.py:16
  1218.0 2.5 collective-permute-start.18
  1218.0 5.2 collective-permute-start.19
  1307.4 11.3 collective-permute-start.20
  1309.1 15.1 %collective-permute-start.21 = (f32[6,4]{0,1:T(4,128)S(1)}, f32[6,4]{0,1:T(4,128)S(1)}, u32[]{:S(2)}, u32[]{:S(2)}) collective-permute-start(f32[6,4]{0,1:T(4,128)S(1)} %multiply_add_fusion.19), channel_id=1, source_target_pairs={{4,0},{8,4},{12,8},{16,12},{20,16},{24,20},{28,24},{0,28},{5,1},{9... | collective-permute-start | bytes 296 | tf_op jit(solution)/shard_map/ppermute | solution.py:16
  1342.4 2.5 collective-permute-start.22
  1342.5 5.2 collective-permute-start.23
  1388.5 11.3 collective-permute-start.24
  1389.6 15.8 %collective-permute-start.25 = (f32[6,4]{0,1:T(4,128)S(1)}, f32[6,4]{0,1:T(4,128)S(1)}, u32[]{:S(2)}, u32[]{:S(2)}) collective-permute-start(f32[6,4]{0,1:T(4,128)S(1)} %multiply_add_fusion.18), channel_id=1, source_target_pairs={{4,0},{8,4},{12,8},{16,12},{20,16},{24,20},{28,24},{0,28},{5,1},{9... | collective-permute-start | bytes 296 | tf_op jit(solution)/shard_map/ppermute | solution.py:16
where the time goes:
time: 1410 us
  local copies, waits for them, and re-layouts  843 us (60%)
  blocking collectives  416 us (30%)
  other arithmetic  67 us (5%)
  starting transfers between devices  38.3 us (3%)
  waiting for transfers between devices  31.8 us (2%)
    gather x24, local copies, waits for them, and re-layouts, scan_terms(): chosen = jnp.take_along_axis(target_tiles, spread_lanes, axis=3)  732 us
    psum x6, blocking collectives, global_sum(): return lax.psum(value, ('sub', 'dom'))  238 us
    unnamed x6, blocking collectives  62.2 us
    gather x16, local copies, waits for them, and re-layouts, scan_terms(): picked = jnp.take(points, sources, axis=1)  46.4 us
    add x26, other arithmetic, rotate(): matrix[row_id, 0] * vector[0] + matrix[row_id, 1] * vector[1]  45.1 us
    all_gather x6, blocking collectives, spread_out(): lax.all_gather(own_part, 'dom', axis=1, tiled=True)  44.6 us
    ppermute x26, starting transfers between devices, from_behind(): return lax.ppermute(block, axis, route)  38.3 us
    all_gather x6, blocking collectives, spread_out(): lax.all_gather(pieces[0], 'dom', axis=1, tiled=True)  32.2 us
  transfers between devices with their start and end apart: 26, of which 14 were waited for; matrix products, arithmetic and copies ran while one was open for 1% of the time, Pallas kernels for 0%

commit v1 on v0

v1 whole, which is shorter than its diff:
```python
import functools

import jax
import jax.numpy as jnp
from jax import lax
from jax.experimental import pallas as pl
from jax.experimental.pallas import tpu as pltpu
from jax.sharding import PartitionSpec as P

CG_ITERS = 2
GN_ITERS = 2
LANES = 128
ROWS = 8
AXES = ("sub", "dom")

SYM3 = [(0, 0), (0, 1), (0, 2), (1, 1), (1, 2), (2, 2)]
SYM4 = [(a, b) for a in range(4) for b in range(a, 4)]
N_MOMENTS = len(SYM4) * len(SYM3) + 4 * 3


def at3(a, b):
    return SYM3.index((min(a, b), max(a, b)))


def at4(a, b):
    return SYM4.index((min(a, b), max(a, b)))


def vmem():
    return pl.BlockSpec(memory_space=pltpu.VMEM)


def smem():
    return pl.BlockSpec(memory_space=pltpu.SMEM)


def pack_body(boundary_ref, out_ref):
    count = out_ref.shape[0]
    part = [boundary_ref[:, :, c, :].reshape(count, LANES) for c in range(6)]
    for c in range(3):
        out_ref[:, c, :] = part[3 + c]
    out_ref[:, 3, :] = part[0] * part[3] + part[1] * part[4] + part[2] * part[5]


def pick_body(points_ref, index_ref, out_ref):
    scans, edges, tiles, _ = index_ref.shape
    per_scan = edges * tiles // ROWS
    edges_here = edges // per_scan
    groups = points_ref.shape[2] // LANES
    for s in range(scans):
        for v in range(per_scan):
            index = index_ref[s, v * edges_here : (v + 1) * edges_here].reshape(ROWS, LANES)
            group = index // LANES
            lane = index % LANES
            found = [jnp.zeros((ROWS, LANES), jnp.float32) for _ in range(3)]
            for g in range(groups):
                here = group == g
                for c in range(3):
                    row = points_ref[s, c : c + 1, g * LANES : (g + 1) * LANES]
                    table = jnp.broadcast_to(row, (ROWS, LANES))
                    found[c] = jnp.where(
                        here, jnp.take_along_axis(table, lane, axis=1), found[c]
                    )
            for c in range(3):
                out_ref[c, s * per_scan + v] = found[c]


def moment_body(
    target_ref, tile_ref, anchor_ref, points_ref, lane_ref, window_ref, out_ref, table_ref
):
    scans, edges, tiles, _ = lane_ref.shape
    bnd = window_ref.shape[0] // (3 * scans * lax.axis_size("dom"))
    per_scan = edges * tiles // ROWS
    edges_here = edges // per_scan
    lane_groups = out_ref.shape[1]
    for s in range(scans):
        for j in range(edges):
            for c in range(tiles):
                row = j * tiles + c
                which = target_ref[s, j] * bnd + tile_ref[s, j, c]
                table_ref[s * per_scan + row // ROWS, :, row % ROWS, :] = window_ref[which]
    lane_at = lax.broadcasted_iota(jnp.int32, (ROWS, LANES), 1)
    row_at = lax.broadcasted_iota(jnp.int32, (ROWS, LANES), 0)
    scale = 1.0 / (tiles * LANES)
    lines = [[] for _ in range(lane_groups)]
    for s in range(scans):
        gathered = [jnp.zeros((ROWS, LANES), jnp.float32) for _ in range(lane_groups)]
        for v in range(per_scan):
            at = s * per_scan + v
            lanes = lane_ref[s, v * edges_here : (v + 1) * edges_here].reshape(ROWS, LANES)
            got = [jnp.take_along_axis(table_ref[at, c], lanes, axis=1) for c in range(4)]
            point = [points_ref[c, at] for c in range(3)] + [None]
            pairs = [got[a] * got[b] for a, b in SYM3]
            weighted = [got[a] * got[3] for a in range(3)]
            place = lane_at - (v * edges_here + row_at // tiles)
            slot = 0
            for a, b in SYM4:
                if a == 3:
                    factor = None
                elif b == 3:
                    factor = point[a]
                else:
                    factor = point[a] * point[b]
                for pair in pairs:
                    value = pair if factor is None else factor * pair
                    total = jnp.sum(value, axis=1, keepdims=True)
                    g, off = divmod(slot * edges, LANES)
                    gathered[g] = jnp.where(place == off, total, gathered[g])
                    slot += 1
            for a in range(4):
                for c in range(3):
                    value = weighted[c] if a == 3 else point[a] * weighted[c]
                    total = jnp.sum(value, axis=1, keepdims=True)
                    g, off = divmod(slot * edges, LANES)
                    gathered[g] = jnp.where(place == off, total, gathered[g])
                    slot += 1
        flat = [jnp.sum(part, axis=0, keepdims=True) * scale for part in gathered]
        lane_row = lax.broadcasted_iota(jnp.int32, (1, LANES), 1)
        for j in range(edges):
            g, off = divmod(N_MOMENTS * edges + j, LANES)
            flat[g] = jnp.where(lane_row == off, target_ref[s, j].astype(jnp.float32), flat[g])
        g, off = divmod((N_MOMENTS + 1) * edges, LANES)
        flat[g] = jnp.where(lane_row == off, anchor_ref[s], flat[g])
        for g in range(lane_groups):
            lines[g].append(flat[g])
    for g in range(lane_groups):
        block = jnp.concatenate(lines[g], axis=0)
        for d in range(out_ref.shape[0]):
            out_ref[d, g] = block


def rotate_sym(matrix, moments):
    half = [
        [sum_of(matrix[a][m] * moments[at3(m, k)] for m in range(3)) for k in range(3)]
        for a in range(3)
    ]
    return [sum_of(half[a][k] * matrix[b][k] for k in range(3)) for a, b in SYM3]


def sum_of(terms):
    total = None
    for term in terms:
        total = term if total is None else total + term
    return total


def edge_terms(moments, own, far):
    place = [[own[3 * a + k] for k in range(3)] + [own[9 + a]] for a in range(3)]
    turn = [[far[3 * a + m] for m in range(3)] for a in range(3)]
    shift = far[9:12]
    turned = [
        rotate_sym(turn, moments[len(SYM3) * k : len(SYM3) * (k + 1)]) for k in range(len(SYM4))
    ]
    nn = turned[at4(3, 3)]
    pnn = []
    ppnn = []
    for e in range(len(SYM3)):
        half = [
            [
                sum_of(place[a][k] * turned[at4(k, l)][e] for k in range(4))
                for l in range(4)
            ]
            for a in range(3)
        ]
        pnn.append([half[a][3] for a in range(3)])
        ppnn.append([sum_of(half[a][l] * place[b][l] for l in range(4)) for a, b in SYM3])

    def pn(a, c, d):
        return pnn[at3(c, d)][a]

    def pp(a, b, c, d):
        return ppnn[at3(c, d)][at3(a, b)]

    mixed = moments[len(SYM4) * len(SYM3) :]
    wx = [
        [sum_of(turn[c][m] * mixed[3 * k + m] for m in range(3)) for c in range(3)]
        for k in range(4)
    ]
    pw = [[sum_of(place[a][k] * wx[k][c] for k in range(4)) for c in range(3)] for a in range(3)]
    nw = wx[3]
    nxt = [(1, 2), (2, 0), (0, 1)]
    block = [[None] * 6 for _ in range(6)]
    for i, (j, k) in enumerate(nxt):
        for i2, (j2, k2) in enumerate(nxt):
            if i2 >= i:
                block[i][i2] = (
                    pp(j, j2, k, k2) - pp(j, k2, k, j2) - pp(k, j2, j, k2) + pp(k, k2, j, j2)
                )
        for d in range(3):
            block[i][3 + d] = pn(j, k, d) - pn(k, j, d)
    for a, b in SYM3:
        block[3 + a][3 + b] = nn[at3(a, b)]
    for a in range(6):
        for b in range(a):
            block[a][b] = block[b][a]
    slopes = []
    for i, (j, k) in enumerate(nxt):
        value = pw[j][k] - pw[k][j]
        for d in range(3):
            value = value + block[i][3 + d] * shift[d]
            value = value - (pp(j, d, k, d) - pp(k, d, j, d))
        slopes.append(value)
    for i in range(3):
        value = nw[i]
        for d in range(3):
            value = value + nn[at3(i, d)] * shift[d] - pn(d, i, d)
        slopes.append(value)
    return block, slopes


def moved(pose, step):
    first, second, third = (0.5 * step[i] for i in range(3))
    length_sq = first * first + second * second + third * third
    inverse = 1.0 / (1.0 + length_sq)
    trace = 1.0 - length_sq
    turn = [
        [
            trace + 2.0 * first * first,
            2.0 * first * second - 2.0 * third,
            2.0 * first * third + 2.0 * second,
        ],
        [
            2.0 * first * second + 2.0 * third,
            trace + 2.0 * second * second,
            2.0 * second * third - 2.0 * first,
        ],
        [
            2.0 * first * third - 2.0 * second,
            2.0 * second * third + 2.0 * first,
            trace + 2.0 * third * third,
        ],
    ]
    turn = [[entry * inverse for entry in line] for line in turn]
    out = [
        sum_of(turn[a][k] * pose[3 * k + c] for k in range(3)) for a in range(3) for c in range(3)
    ]
    out += [sum_of(turn[a][k] * pose[9 + k] for k in range(3)) + step[3 + a] for a in range(3)]
    return out


def solve_body(first_ref, pose_ref, rows_ref, out_ref, *, edges, scan_sub):
    devices, lane_groups, scan_dev, _ = rows_ref.shape
    scans = devices * scan_dev
    chunks = scans // LANES
    blocks = [rows_ref[:, g].reshape(scans, LANES) for g in range(lane_groups)]
    columns = [part.T for part in blocks]

    def plane(slot, height=edges):
        g, off = divmod(slot * edges, LANES)
        return columns[g][off : off + height]

    def end_of(slots, scan):
        end = (scan // scan_sub) * scan_sub + slots - scan_sub
        end = jnp.where(end < 0, end + scans, end)
        return jnp.where(end >= scans, end - scans, end)

    moments = [plane(k) for k in range(N_MOMENTS)]
    end = end_of(
        plane(N_MOMENTS).astype(jnp.int32), lax.broadcasted_iota(jnp.int32, (edges, scans), 1)
    )
    anchor = plane(N_MOMENTS + 1, 1)
    g, off = divmod(N_MOMENTS * edges, LANES)
    hot = []
    for j in range(edges):
        slots = blocks[g][:, off + j : off + j + 1].astype(jnp.int32)
        down = end_of(slots, lax.broadcasted_iota(jnp.int32, (scans, 1), 0))
        across = lax.broadcasted_iota(jnp.int32, (scans, scans), 1)
        hot.append((down == across).astype(jnp.bfloat16))

    def at_end(line):
        wide = []
        for o in range(chunks):
            index = end[:, o * LANES : (o + 1) * LANES]
            found = None
            for q in range(chunks):
                table = jnp.broadcast_to(line[:, q * LANES : (q + 1) * LANES], (edges, LANES))
                value = jnp.take_along_axis(table, index % LANES, axis=1)
                found = value if found is None else jnp.where(index // LANES == q, value, found)
            wide.append(found)
        return wide[0] if chunks == 1 else jnp.concatenate(wide, axis=1)

    def to_end(planes):
        full = jnp.concatenate(planes, axis=0)
        high = full.astype(jnp.bfloat16)
        rest = full - high.astype(jnp.float32)
        middle = rest.astype(jnp.bfloat16)
        low = (rest - middle.astype(jnp.float32)).astype(jnp.bfloat16)
        pieces = jnp.concatenate([high, middle, low], axis=0)
        count = full.shape[0]
        row = lax.broadcasted_iota(jnp.int32, (count, scans), 0) % edges
        total = jnp.zeros((count, scans), jnp.float32)
        for j in range(edges):
            part = jnp.dot(pieces, hot[j], preferred_element_type=jnp.float32)
            part = part[:count] + part[count : 2 * count] + part[2 * count :]
            total = jnp.where(row == j, part, total)
        return [
            jnp.sum(total[edges * i : edges * (i + 1)], axis=0, keepdims=True)
            for i in range(len(planes))
        ]

    def over_edges(value):
        return jnp.sum(value, axis=0, keepdims=True)

    def stack(lines):
        return jnp.concatenate(lines, axis=0)

    def full_sum(value):
        return jnp.sum(jnp.sum(value, axis=0, keepdims=True), axis=1, keepdims=True)

    pose = [pose_ref[i : i + 1, :] for i in range(12)]
    for _ in range(GN_ITERS):
        block, slopes = edge_terms(moments, pose, [at_end(line) for line in pose])
        diag = [block[a][a] for a in range(6)]
        sums = to_end(slopes + diag)
        residual = stack([over_edges(slopes[a]) - sums[a] for a in range(6)])
        diagonal = stack([over_edges(diag[a]) + sums[6 + a] + anchor for a in range(6)])

        def image_of(vector, block=block):
            lines = [vector[a : a + 1] for a in range(6)]
            spread = [line - at_end(line) for line in lines]
            pushed = [sum_of(block[a][b] * spread[b] for b in range(6)) for a in range(6)]
            back = to_end(pushed)
            return stack(
                [anchor * lines[a] + over_edges(pushed[a]) - back[a] for a in range(6)]
            )

        scaled = residual / diagonal
        direction = scaled
        energy = full_sum(residual * scaled)
        increment = jnp.zeros_like(residual)
        for sweep in range(CG_ITERS):
            image = image_of(direction)
            step = energy / full_sum(direction * image)
            increment = increment + step * direction
            if sweep + 1 < CG_ITERS:
                residual = residual - step * image
                scaled = residual / diagonal
                renewed = full_sum(residual * scaled)
                direction = scaled + (renewed / energy) * direction
                energy = renewed
        pose = moved(pose, [increment[a : a + 1] for a in range(6)])
    final = stack(pose)
    lane_at = lax.broadcasted_iota(jnp.int32, final.shape, 1)
    out_at = lax.broadcasted_iota(jnp.int32, out_ref.shape, 1)
    result = jnp.zeros(out_ref.shape, jnp.float32)
    for s in range(scan_dev):
        column = jnp.sum(
            jnp.where(lane_at == first_ref[0] + s, final, 0.0), axis=1, keepdims=True
        )
        result = jnp.where(out_at == s, column, result)
    out_ref[...] = result


def local(source_points, boundary, poses, anchor, edge_target, corr_tile, corr_source, corr_lane):
    scan_dev, bnd = boundary.shape[:2]
    edges, tiles = corr_tile.shape[1:]
    doms = lax.axis_size("dom")
    subs = lax.axis_size("sub")
    devices = subs * doms
    scan_sub = scan_dev * doms
    vectors = scan_dev * edges * tiles // ROWS
    lane_groups = -(-((N_MOMENTS + 2) * edges) // LANES)

    packed = pl.pallas_call(
        pack_body,
        out_shape=jax.ShapeDtypeStruct((scan_dev * bnd, 4, LANES), jnp.float32),
        in_specs=[vmem()],
        out_specs=vmem(),
        name="pack",
    )(boundary)
    before = lax.ppermute(packed, "sub", [((i - 1) % subs, i) for i in range(subs)])
    beyond = lax.ppermute(packed, "sub", [((i + 1) % subs, i) for i in range(subs)])
    picked = pl.pallas_call(
        pick_body,
        out_shape=jax.ShapeDtypeStruct((3, vectors, ROWS, LANES), jnp.float32),
        in_specs=[vmem(), vmem()],
        out_specs=vmem(),
        name="pick",
    )(source_points, corr_source)
    window = lax.all_gather(jnp.stack([before, packed, beyond]), "dom", axis=1, tiled=True)
    window = window.reshape(3 * scan_sub * bnd, 4, LANES)
    rows = pl.pallas_call(
        moment_body,
        out_shape=jax.ShapeDtypeStruct((devices, lane_groups, scan_dev, LANES), jnp.float32),
        in_specs=[smem(), smem(), smem(), vmem(), vmem(), vmem()],
        out_specs=vmem(),
        scratch_shapes=[pltpu.VMEM((vectors, 4, ROWS, LANES), jnp.float32)],
        name="moments",
    )(edge_target, corr_tile, anchor, picked, corr_lane, window)
    rows = lax.all_to_all(rows, AXES, 0, 0)
    first = (lax.axis_index(AXES) * scan_dev).astype(jnp.int32).reshape(1)
    return pl.pallas_call(
        functools.partial(solve_body, edges=edges, scan_sub=scan_sub),
        out_shape=jax.ShapeDtypeStruct((12, scan_dev), jnp.float32),
        in_specs=[smem(), vmem(), vmem()],
        out_specs=vmem(),
        name="solve",
    )(first, poses, rows)


def solution(mesh):
    in_specs = (
        P(AXES, None, None),
        P(AXES, None, None, None),
        P(),
        P(AXES),
        P(AXES, None),
        P(AXES, None, None),
        P(AXES, None, None, None),
        P(AXES, None, None, None),
    )
    out_specs = P(None, AXES)
    return jax.shard_map(local, mesh=mesh, in_specs=in_specs, out_specs=out_specs, check_vma=False)
```

time: 1410 us -> 47.3 us (0.03)
  local copies, waits for them, and re-layouts: 843 us -> 4.47 us
  blocking collectives: 416 us -> 11 us
  other arithmetic: 67 us -> 0.05 us
  starting transfers between devices: 38.3 us -> 7.44 us
  waiting for transfers between devices: 31.8 us -> 12 us
    gather x68 -> x0, local copies, waits for them, and re-layouts: 805 us -> none  [the longest x24 732 us: scan_terms(): chosen = jnp.take_along_axis(target_tiles, spread_lanes, axis=3)]
    psum x6 -> x0, blocking collectives: 238 us -> none  [global_sum(): return lax.psum(value, ('sub', 'dom'))]
    all_gather x19 -> x1, blocking collectives: 116 us -> 11 us  [local(): lax.all_gather(jnp.stack([before, packed, beyond]), 'dom', axis=1, tiled=...]
    unnamed x6 -> x0, blocking collectives: 62.2 us -> none
    add x60 -> x0, other arithmetic: 46.4 us -> none  [the longest x26 45.1 us: rotate(): matrix[row_id, 0] * vector[0] + matrix[row_id, 1] * vector[1]]
    ppermute x26 -> x2, starting transfers between devices: 38.3 us -> 5.1 us  [the longest x1 5.1 us: local(): lax.ppermute(packed, 'sub', [((i + 1) % subs, i) for i in range(subs)])]
    ppermute x26 -> x2, waiting for transfers between devices: 31.8 us -> 2.63 us  [the longest x1 2.63 us: local(): lax.ppermute(packed, 'sub', [((i - 1) % subs, i) for i in range(subs)])]
  transfers between devices with their start and end apart: 26 -> 3, of which waited for: 14 -> 2; matrix products, arithmetic and copies ran while one was open for 1% -> 2% of each run, Pallas kernels for 0% -> 5%
where the time goes in v1:
time: 47.3 us; the launch traced here: 47 us
  Pallas kernels  12 us (25%)
  waiting for transfers between devices  12 us (25%)
  blocking collectives  11 us (23%)
  starting transfers between devices  7.44 us (16%)
  local copies, waits for them, and re-layouts  4.47 us (9%)
    all_gather x1, blocking collectives, local(): lax.all_gather(jnp.stack([before, packed, beyond]), 'dom', axis=1, tiled=...  11 us
    all_to_all x1, waiting for transfers between devices, local(): rows = lax.all_to_all(rows, AXES, 0, 0)  9.33 us
    ppermute x1, starting transfers between devices, local(): lax.ppermute(packed, 'sub', [((i + 1) % subs, i) for i in range(subs)])  5.1 us
    pallas_call x1, Pallas kernels, local(): pl.pallas_call(functools.partial(solve_body, edges=edges, scan_sub=scan_s...  4.47 us
    pallas_call x1, Pallas kernels, local(): pl.pallas_call(moment_body, out_shape=jax.ShapeDtypeStruct((devices, lane...  3.46 us
    unnamed x8, local copies, waits for them, and re-layouts  3.12 us
    ppermute x1, waiting for transfers between devices, local(): lax.ppermute(packed, 'sub', [((i - 1) % subs, i) for i in range(subs)])  2.63 us
    pallas_call x1, Pallas kernels, local(): pl.pallas_call(pick_body, out_shape=jax.ShapeDtypeStruct((3, vectors, ROW...  2.54 us
  transfers between devices with their start and end apart: 3, of which 2 were waited for; matrix products, arithmetic and copies ran while one was open for 2% of the time, Pallas kernels for 5%

profile of v1, /device:TPU:1, one launch (start us, length us, event | category | flops | bytes accessed | tf_op | source)
XLA Modules:
  0.0 47.0 jit_solution(3827143684730384241)
XLA Ops:
  0.0 0.0 copy-start.2
  0.0 1.6 %copy.10.boundary_ref = f32[4,8,6,128]{3,2,1,0:T(8,128)} copy(f32[4,8,6,128]{3,1,2,0:T(8,128)} %param.9) | data formatting | bytes 196608 | tf_op args[1]
  1.6 1.6 %pack.1 = f32[32,4,128]{2,1,0:T(4,128)} custom-call(f32[4,8,6,128]{3,2,1,0:T(8,128)} %copy.10.boundary_ref), custom_call_target="tpu_custom_call" | custom-call | tf_op jit(solution)/shard_map/pack/pallas_call | solution.py:364
  3.2 5.1 %collective-permute-start.1 = (f32[32,4,128]{2,1,0:T(4,128)}, f32[32,4,128]{2,1,0:T(4,128)S(1)}, u32[]{:S(2)}, u32[]{:S(2)}) collective-permute-start(f32[32,4,128]{2,1,0:T(4,128)} %pack.1), channel_id=1, source_target_pairs={{4,0},{8,4},{12,8},{16,12},{20,16},{24,20},{28,24},{0,28},{5,1},{9... | collective-permute-start | bytes 196616 | tf_op jit(solution)/shard_map/ppermute | solution.py:372
  8.3 0.0 collective-permute-start
  8.3 0.0 copy-done.2
  8.3 0.8 %copy.9.points_ref = f32[4,3,4096]{2,1,0:T(4,128)} copy(f32[4,3,4096]{2,0,1:T(4,128)S(1)} %copy-done.2) | data formatting | bytes 393216 | tf_op args[0]
  9.1 0.0 copy-start.1
  9.1 2.5 %pick.1.points_ref = f32[3,8,8,128]{3,2,1,0:T(8,128)} custom-call(f32[4,3,4096]{2,1,0:T(4,128)} %copy.9.points_ref, s32[4,4,4,128]{3,2,1,0:T(4,128)} %index_ref.1), custom_call_target="tpu_custom_call" | custom-call | tf_op jit(solution)/shard_map/pick/pallas_call | solution.py:373
  11.7 0.0 collective-permute-done.1
  11.7 2.6 %collective-permute-done = f32[32,4,128]{2,1,0:T(4,128)S(1)} collective-permute-done((f32[32,4,128]{2,1,0:T(4,128)}, f32[32,4,128]{2,1,0:T(4,128)S(1)}, u32[]{:S(2)}, u32[]{:S(2)}) %collective-permute-start) | collective-permute-done | bytes 65568 | tf_op jit(solution)/shard_map/ppermute | solution.py:371
  14.3 0.0 copy-done.1
  14.4 11.0 %all_gather.3 = f32[3,128,4,128]{3,2,1,0:T(4,128)} all-gather(f32[3,32,4,128]{3,2,1,0:T(4,128)S(1)} %pad_maximum_fusion), channel_id=1, replica_groups=mesh['sub'=8,'dom'=4] {'dom'}, dimensions={1}, use_global_device_ids=true | all-gather | bytes 983040 | tf_op jit(solution)/shard_map/all_gather | solution.py:380
  25.4 3.5 %moments.1 = f32[32,3,4,128]{3,2,1,0:T(4,128)} custom-call(s32[4,4]{1,0:T(4,128)} %target_ref.1, s32[4,4,4]{2,1,0:T(4,128)} %tile_ref.1, f32[4]{0:T(128)} %anchor_ref.1, f32[3,8,8,128]{3,2,1,0:T(8,128)} %pick.1.points_ref, s32[4,4,4,128]{3,2,1,0:T(4,128)} %lane_ref.1, f32[384,4,128]{2,1,0:T(4,128)} %bitcast.5), custom_call_target="tpu_custom_call" | custom-call | tf_op jit(solution)/shard_map/moments/pallas_call | solution.py:382
  28.8 2.3 %all-to-all-start = ((f32[32,3,4,128]{3,2,1,0:T(4,128)}), f32[32,3,4,128]{3,2,1,0:T(4,128)S(1)}, u32[]{:S(2)}, u32[]{:S(2)}) async-start(f32[32,3,4,128]{3,2,1,0:T(4,128)} %moments.1), calls=%async_computation | async-start | bytes 393216 | tf_op jit(solution)/shard_map/all_to_all | solution.py:390
  31.2 9.3 %all-to-all-done.rows_ref = f32[32,3,4,128]{3,2,1,0:T(4,128)S(1)} async-done(((f32[32,3,4,128]{3,2,1,0:T(4,128)}), f32[32,3,4,128]{3,2,1,0:T(4,128)S(1)}, u32[]{:S(2)}, u32[]{:S(2)}) %all-to-all-start) | async-done | bytes 196640 | tf_op jit(solution)/shard_map/all_to_all | solution.py:390
  40.5 0.0 copy-start
  40.5 0.7 %copy-done = f32[32,3,4,128]{3,2,1,0:T(4,128)} copy-done((f32[32,3,4,128]{3,2,1,0:T(4,128)}, f32[32,3,4,128]{3,2,1,0:T(4,128)S(1)}, u32[]{:S(2)}) %copy-start) | copy-done | bytes 196632
  41.2 4.5 %solve.1 = f32[12,4]{1,0:T(8,128)} custom-call(s32[1]{0:T(128)} %bitcast.first_ref, f32[12,128]{1,0:T(8,128)} %pose_ref.1, f32[32,3,4,128]{3,2,1,0:T(4,128)} %copy-done), custom_call_target="tpu_custom_call" | custom-call | tf_op jit(solution)/shard_map/solve/pallas_call | solution.py:392
  45.6 1.4 %copy.11 = f32[12,4]{0,1:T(4,128)} copy(f32[12,4]{1,0:T(8,128)} %solve.1) | data formatting | bytes 384 | tf_op jit(solution)/shard_map/solve/pallas_call | solution.py:392
  (1 shorter events, 0.0 us)
Async XLA Ops:
  0.0 8.3 %copy-start.2 = (f32[4,3,4096]{2,0,1:T(4,128)S(1)}, f32[4,3,4096]{2,0,1:T(4,128)}, u32[]{:S(2)}) copy-start(f32[4,3,4096]{2,0,1:T(4,128)} %param.8) | copy-start | bytes 589828
  3.2 8.5 %collective-permute-start.1 = (f32[32,4,128]{2,1,0:T(4,128)}, f32[32,4,128]{2,1,0:T(4,128)S(1)}, u32[]{:S(2)}, u32[]{:S(2)}) collective-permute-start(f32[32,4,128]{2,1,0:T(4,128)} %pack.1), channel_id=1, source_target_pairs={{4,0},{8,4},{12,8},{16,12},{20,16},{24,20},{28,24},{0,28},{5,1},{9... | collective-permute-start | bytes 196616 | tf_op jit(solution)/shard_map/ppermute | solution.py:372
  8.3 6.0 %collective-permute-start = (f32[32,4,128]{2,1,0:T(4,128)}, f32[32,4,128]{2,1,0:T(4,128)S(1)}, u32[]{:S(2)}, u32[]{:S(2)}) collective-permute-start(f32[32,4,128]{2,1,0:T(4,128)} %pack.1), channel_id=1, source_target_pairs={{28,0},{0,4},{4,8},{8,12},{12,16},{16,20},{20,24},{24,28},{29,1},{... | collective-permute-start | bytes 196616 | tf_op jit(solution)/shard_map/ppermute | solution.py:371
  9.1 5.2 %copy-start.1 = (f32[32,4,128]{2,1,0:T(4,128)S(1)}, f32[32,4,128]{2,1,0:T(4,128)}, u32[]{:S(2)}) copy-start(f32[32,4,128]{2,1,0:T(4,128)} %pack.1) | copy-start | bytes 196612
  28.8 11.7 %all-to-all-start = ((f32[32,3,4,128]{3,2,1,0:T(4,128)}), f32[32,3,4,128]{3,2,1,0:T(4,128)S(1)}, u32[]{:S(2)}, u32[]{:S(2)}) async-start(f32[32,3,4,128]{3,2,1,0:T(4,128)} %moments.1), calls=%async_computation | async-start | bytes 393216 | tf_op jit(solution)/shard_map/all_to_all | solution.py:390
  40.5 0.7 %copy-start = (f32[32,3,4,128]{3,2,1,0:T(4,128)}, f32[32,3,4,128]{3,2,1,0:T(4,128)S(1)}, u32[]{:S(2)}) copy-start(f32[32,3,4,128]{3,2,1,0:T(4,128)S(1)} %all-to-all-done.rows_ref) | copy-start | bytes 589828

commit v2 on v1

--- a/solution.py
+++ b/solution.py
@@ -34,12 +34,17 @@
     return pl.BlockSpec(memory_space=pltpu.SMEM)
 
 
+def in_vmem(array):
+    return pltpu.with_memory_space_constraint(array, pltpu.VMEM)
+
+
 def pack_body(boundary_ref, out_ref):
-    count = out_ref.shape[0]
-    part = [boundary_ref[:, :, c, :].reshape(count, LANES) for c in range(6)]
-    for c in range(3):
-        out_ref[:, c, :] = part[3 + c]
-    out_ref[:, 3, :] = part[0] * part[3] + part[1] * part[4] + part[2] * part[5]
+    bnd = boundary_ref.shape[2]
+    for s in range(boundary_ref.shape[0]):
+        part = [boundary_ref[s, c] for c in range(6)]
+        part.append(part[0] * part[3] + part[1] * part[4] + part[2] * part[5])
+        for c in range(4):
+            out_ref[s * bnd : (s + 1) * bnd, c, :] = part[3 + c]
 
 
 def pick_body(points_ref, index_ref, out_ref):
@@ -56,7 +61,7 @@
             for g in range(groups):
                 here = group == g
                 for c in range(3):
-                    row = points_ref[s, c : c + 1, g * LANES : (g + 1) * LANES]
+                    row = points_ref[c, s : s + 1, g * LANES : (g + 1) * LANES]
                     table = jnp.broadcast_to(row, (ROWS, LANES))
                     found[c] = jnp.where(
                         here, jnp.take_along_axis(table, lane, axis=1), found[c]
@@ -341,14 +346,14 @@
         pose = moved(pose, [increment[a : a + 1] for a in range(6)])
     final = stack(pose)
     lane_at = lax.broadcasted_iota(jnp.int32, final.shape, 1)
-    out_at = lax.broadcasted_iota(jnp.int32, out_ref.shape, 1)
-    result = jnp.zeros(out_ref.shape, jnp.float32)
+    out_at = lax.broadcasted_iota(jnp.int32, (12, scan_dev), 1)
+    result = jnp.zeros((12, scan_dev), jnp.float32)
     for s in range(scan_dev):
         column = jnp.sum(
             jnp.where(lane_at == first_ref[0] + s, final, 0.0), axis=1, keepdims=True
         )
         result = jnp.where(out_at == s, column, result)
-    out_ref[...] = result
+    out_ref[...] = result.T
 
 
 def local(source_points, boundary, poses, anchor, edge_target, corr_tile, corr_source, corr_lane):
@@ -363,39 +368,39 @@
 
     packed = pl.pallas_call(
         pack_body,
-        out_shape=jax.ShapeDtypeStruct((scan_dev * bnd, 4, LANES), jnp.float32),
+        out_shape=pltpu.VMEM((scan_dev * bnd, 4, LANES), jnp.float32),
         in_specs=[vmem()],
         out_specs=vmem(),
         name="pack",
-    )(boundary)
+    )(boundary.transpose(0, 2, 1, 3))
     before = lax.ppermute(packed, "sub", [((i - 1) % subs, i) for i in range(subs)])
     beyond = lax.ppermute(packed, "sub", [((i + 1) % subs, i) for i in range(subs)])
     picked = pl.pallas_call(
         pick_body,
-        out_shape=jax.ShapeDtypeStruct((3, vectors, ROWS, LANES), jnp.float32),
+        out_shape=pltpu.VMEM((3, vectors, ROWS, LANES), jnp.float32),
         in_specs=[vmem(), vmem()],
         out_specs=vmem(),
         name="pick",
-    )(source_points, corr_source)
+    )(source_points.transpose(1, 0, 2), corr_source)
     window = lax.all_gather(jnp.stack([before, packed, beyond]), "dom", axis=1, tiled=True)
     window = window.reshape(3 * scan_sub * bnd, 4, LANES)
     rows = pl.pallas_call(
         moment_body,
-        out_shape=jax.ShapeDtypeStruct((devices, lane_groups, scan_dev, LANES), jnp.float32),
+        out_shape=pltpu.VMEM((devices, lane_groups, scan_dev, LANES), jnp.float32),
         in_specs=[smem(), smem(), smem(), vmem(), vmem(), vmem()],
         out_specs=vmem(),
         scratch_shapes=[pltpu.VMEM((vectors, 4, ROWS, LANES), jnp.float32)],
         name="moments",
-    )(edge_target, corr_tile, anchor, picked, corr_lane, window)
+    )(edge_target, corr_tile, anchor, in_vmem(picked), corr_lane, in_vmem(window))
     rows = lax.all_to_all(rows, AXES, 0, 0)
     first = (lax.axis_index(AXES) * scan_dev).astype(jnp.int32).reshape(1)
     return pl.pallas_call(
         functools.partial(solve_body, edges=edges, scan_sub=scan_sub),
-        out_shape=jax.ShapeDtypeStruct((12, scan_dev), jnp.float32),
+        out_shape=jax.ShapeDtypeStruct((scan_dev, 12), jnp.float32),
         in_specs=[smem(), vmem(), vmem()],
         out_specs=vmem(),
         name="solve",
-    )(first, poses, rows)
+    )(first, poses, in_vmem(rows)).T
 
 
 def solution(mesh):

time: 47.3 us -> 39.8 us (0.84)
  local copies, waits for them, and re-layouts: 4.47 us -> 0 us
  waiting for transfers between devices: 12 us -> 9.2 us
  starting transfers between devices: 7.44 us -> 9.97 us
  Pallas kernels: 12 us -> 10.1 us
  blocking collectives: 11 us -> 10.1 us
    unnamed x8 -> x0, local copies, waits for them, and re-layouts: 3.12 us -> none
    ppermute x1, waiting for transfers between devices: 2.63 us -> 0.01 us  [local(): lax.ppermute(packed, 'sub', [((i - 1) % subs, i) for i in range(subs)])]
    all_to_all x1, starting transfers between devices: 2.34 us -> 4.76 us  [local(): rows = lax.all_to_all(rows, AXES, 0, 0)]
    ppermute x1, starting transfers between devices: 0.01 us -> 2.11 us  [local(): lax.ppermute(packed, 'sub', [((i - 1) % subs, i) for i in range(subs)])]
    ppermute x1, starting transfers between devices: 5.1 us -> 3.1 us  [local(): lax.ppermute(packed, 'sub', [((i + 1) % subs, i) for i in range(subs)])]
    pallas_call x3, Pallas kernels: 7.58 us -> 5.85 us  [the longest x1 3.06 us: local(): pl.pallas_call(moment_body, out_shape=pltpu.VMEM((devices, lane_groups, s...]
    pallas_call x1 -> x0, local copies, waits for them, and re-layouts: 1.35 us -> none  [local(): pl.pallas_call(functools.partial(solve_body, edges=edges, scan_sub=scan_s...]
    all_gather x1, blocking collectives: 11 us -> 10.1 us  [local(): lax.all_gather(jnp.stack([before, packed, beyond]), 'dom', axis=1, tiled=...]
  transfers between devices with their start and end apart: 3 -> 3, of which waited for: 2 -> 1; matrix products, arithmetic and copies ran while one was open for 2% -> 0% of each run, Pallas kernels for 5% -> 5%
where the time goes in v2:
time: 39.8 us; the launch traced here: 39.5 us
  Pallas kernels  10.1 us (25%)
  blocking collectives  10.1 us (25%)
  starting transfers between devices  9.97 us (25%)
  waiting for transfers between devices  9.2 us (23%)
    all_gather x1, blocking collectives, local(): lax.all_gather(jnp.stack([before, packed, beyond]), 'dom', axis=1, tiled=...  10.1 us
    all_to_all x1, waiting for transfers between devices, local(): rows = lax.all_to_all(rows, AXES, 0, 0)  9.2 us
    all_to_all x1, starting transfers between devices, local(): rows = lax.all_to_all(rows, AXES, 0, 0)  4.76 us
    pallas_call x1, Pallas kernels, local(): pl.pallas_call(functools.partial(solve_body, edges=edges, scan_sub=scan_s...  4.27 us
    ppermute x1, starting transfers between devices, local(): lax.ppermute(packed, 'sub', [((i + 1) % subs, i) for i in range(subs)])  3.1 us
    pallas_call x1, Pallas kernels, local(): pl.pallas_call(moment_body, out_shape=pltpu.VMEM((devices, lane_groups, s...  3.06 us
    ppermute x1, starting transfers between devices, local(): lax.ppermute(packed, 'sub', [((i - 1) % subs, i) for i in range(subs)])  2.11 us
    pallas_call x1, Pallas kernels, local(): pl.pallas_call(pick_body, out_shape=pltpu.VMEM((3, vectors, ROWS, LANES),...  1.85 us
  transfers between devices with their start and end apart: 3, of which 1 were waited for; matrix products, arithmetic and copies ran while one was open for 0% of the time, Pallas kernels for 5%

profile of v2, /device:TPU:1, one launch (start us, length us, event | category | flops | bytes accessed | tf_op | source)
XLA Modules:
  0.0 39.5 jit_solution(15406104232574526300)
XLA Ops:
  0.0 0.9 %pack.1 = f32[32,4,128]{2,1,0:T(4,128)S(1)} custom-call(f32[4,6,8,128]{3,2,1,0:T(8,128)} %bitcast.11), custom_call_target="tpu_custom_call" | custom-call | tf_op jit(solution)/shard_map/pack/pallas_call | solution.py:369
  0.9 2.1 %collective-permute-start = (f32[32,4,128]{2,1,0:T(4,128)S(1)}, f32[32,4,128]{2,1,0:T(4,128)S(1)}, u32[]{:S(2)}, u32[]{:S(2)}) collective-permute-start(f32[32,4,128]{2,1,0:T(4,128)S(1)} %pack.1), channel_id=1, source_target_pairs={{28,0},{0,4},{4,8},{8,12},{12,16},{16,20},{20,24},{24,28},{29,1},{... | collective-permute-start | bytes 196616 | tf_op jit(solution)/shard_map/ppermute | solution.py:376
  3.0 3.1 %collective-permute-start.1 = (f32[32,4,128]{2,1,0:T(4,128)S(1)}, f32[32,4,128]{2,1,0:T(4,128)S(1)}, u32[]{:S(2)}, u32[]{:S(2)}) collective-permute-start(f32[32,4,128]{2,1,0:T(4,128)S(1)} %pack.1), channel_id=1, source_target_pairs={{4,0},{8,4},{12,8},{16,12},{20,16},{24,20},{28,24},{0,28},{5,1},{9... | collective-permute-start | bytes 196616 | tf_op jit(solution)/shard_map/ppermute | solution.py:377
  6.2 1.8 %pick.1.points_ref = f32[3,8,8,128]{3,2,1,0:T(8,128)S(1)} custom-call(f32[3,4,4096]{2,1,0:T(4,128)} %bitcast.10, s32[4,4,4,128]{3,2,1,0:T(4,128)} %index_ref.1), custom_call_target="tpu_custom_call" | custom-call | tf_op jit(solution)/shard_map/pick/pallas_call | solution.py:378
  8.0 0.0 collective-permute-done
  8.0 0.0 collective-permute-done.1
  8.1 10.1 %all_gather.3 = f32[3,128,4,128]{3,2,1,0:T(4,128)S(1)} all-gather(f32[3,32,4,128]{3,2,1,0:T(4,128)S(1)} %pad_maximum_fusion), channel_id=1, replica_groups=mesh['sub'=8,'dom'=4] {'dom'}, dimensions={1}, use_global_device_ids=true | all-gather | bytes 983040 | tf_op jit(solution)/shard_map/all_gather | solution.py:385
  18.2 3.1 %moments.1 = f32[32,3,4,128]{3,2,1,0:T(4,128)} custom-call(s32[4,4]{1,0:T(4,128)} %target_ref.1, s32[4,4,4]{2,1,0:T(4,128)} %tile_ref.1, f32[4]{0:T(128)} %anchor_ref.1, f32[3,8,8,128]{3,2,1,0:T(8,128)S(1)} %pick.1.points_ref, s32[4,4,4,128]{3,2,1,0:T(4,128)} %lane_ref.1, f32[384,4,128]{2,1,0:T(4,128)S(1)} %bitcast.8), custom_call_target="tpu_custom_call" | custom-call | tf_op jit(solution)/shard_map/moments/pallas_call | solution.py:387
  21.2 4.8 %all-to-all-start = ((f32[32,3,4,128]{3,2,1,0:T(4,128)}), f32[32,3,4,128]{3,2,1,0:T(4,128)S(1)}, u32[]{:S(2)}, u32[]{:S(2)}) async-start(f32[32,3,4,128]{3,2,1,0:T(4,128)} %moments.1), calls=%async_computation | async-start | bytes 393216 | tf_op jit(solution)/shard_map/all_to_all | solution.py:395
  26.0 9.2 %all-to-all-done.rows_ref = f32[32,3,4,128]{3,2,1,0:T(4,128)S(1)} async-done(((f32[32,3,4,128]{3,2,1,0:T(4,128)}), f32[32,3,4,128]{3,2,1,0:T(4,128)S(1)}, u32[]{:S(2)}, u32[]{:S(2)}) %all-to-all-start) | async-done | bytes 196640 | tf_op jit(solution)/shard_map/all_to_all | solution.py:395
  35.2 4.3 %solve.1 = f32[4,12]{1,0:T(4,128)} custom-call(s32[1]{0:T(128)} %bitcast.first_ref, f32[12,128]{1,0:T(8,128)} %pose_ref.1, f32[32,3,4,128]{3,2,1,0:T(4,128)S(1)} %all-to-all-done.rows_ref), custom_call_target="tpu_custom_call" | custom-call | tf_op jit(solution)/shard_map/solve/pallas_call | solution.py:397
  (1 shorter events, 0.0 us)
Async XLA Ops:
  0.9 7.1 %collective-permute-start = (f32[32,4,128]{2,1,0:T(4,128)S(1)}, f32[32,4,128]{2,1,0:T(4,128)S(1)}, u32[]{:S(2)}, u32[]{:S(2)}) collective-permute-start(f32[32,4,128]{2,1,0:T(4,128)S(1)} %pack.1), channel_id=1, source_target_pairs={{28,0},{0,4},{4,8},{8,12},{12,16},{16,20},{20,24},{24,28},{29,1},{... | collective-permute-start | bytes 196616 | tf_op jit(solution)/shard_map/ppermute | solution.py:376
  3.0 5.0 %collective-permute-start.1 = (f32[32,4,128]{2,1,0:T(4,128)S(1)}, f32[32,4,128]{2,1,0:T(4,128)S(1)}, u32[]{:S(2)}, u32[]{:S(2)}) collective-permute-start(f32[32,4,128]{2,1,0:T(4,128)S(1)} %pack.1), channel_id=1, source_target_pairs={{4,0},{8,4},{12,8},{16,12},{20,16},{24,20},{28,24},{0,28},{5,1},{9... | collective-permute-start | bytes 196616 | tf_op jit(solution)/shard_map/ppermute | solution.py:377
  21.2 14.0 %all-to-all-start = ((f32[32,3,4,128]{3,2,1,0:T(4,128)}), f32[32,3,4,128]{3,2,1,0:T(4,128)S(1)}, u32[]{:S(2)}, u32[]{:S(2)}) async-start(f32[32,3,4,128]{3,2,1,0:T(4,128)} %moments.1), calls=%async_computation | async-start | bytes 393216 | tf_op jit(solution)/shard_map/all_to_all | solution.py:395

commit v3 on v2

v3 whole, which is shorter than its diff:
```python
import functools

import jax
import jax.numpy as jnp
from jax import lax
from jax.experimental import pallas as pl
from jax.experimental.pallas import tpu as pltpu
from jax.sharding import PartitionSpec as P

CG_ITERS = 2
GN_ITERS = 2
LANES = 128
LANE_BITS = 7
ROWS = 8
AXES = ("sub", "dom")

SYM3 = [(0, 0), (0, 1), (0, 2), (1, 1), (1, 2), (2, 2)]
SYM4 = [(a, b) for a in range(4) for b in range(a, 4)]


def at3(a, b):
    return SYM3.index((min(a, b), max(a, b)))


def at4(a, b):
    return SYM4.index((min(a, b), max(a, b)))


def vmem():
    return pl.BlockSpec(memory_space=pltpu.VMEM)


def smem():
    return pl.BlockSpec(memory_space=pltpu.SMEM)


def in_vmem(array):
    return pltpu.with_memory_space_constraint(array, pltpu.VMEM)


def pack_body(boundary_ref, out_ref):
    bnd = boundary_ref.shape[2]
    for s in range(boundary_ref.shape[0]):
        part = [boundary_ref[s, c] for c in range(6)]
        part.append(part[0] * part[3] + part[1] * part[4] + part[2] * part[5])
        for c in range(4):
            out_ref[s * bnd : (s + 1) * bnd, c, :] = part[3 + c]


def pick_body(points_ref, index_ref, out_ref, table_ref, rows_ref):
    scans, edges, tiles, _ = index_ref.shape
    pack = ROWS // edges
    groups = points_ref.shape[2] // LANES
    row_at = lax.broadcasted_iota(jnp.int32, (ROWS, LANES), 0)
    for s in range(scans):
        for c in range(tiles):
            at = (s // pack) * tiles + c
            rows_ref[at, (s % pack) * edges : (s % pack + 1) * edges] = index_ref[s, :, c, :]
    for p in range(scans // pack):
        for g in range(groups):
            for k in range(3):
                table = None
                for n in range(pack):
                    s = p * pack + n
                    row = points_ref[k, s : s + 1, g * LANES : (g + 1) * LANES]
                    wide = jnp.broadcast_to(row, (ROWS, LANES))
                    table = wide if n == 0 else jnp.where(row_at >= n * edges, wide, table)
                table_ref[p, g * 3 + k] = table
    for p in range(scans // pack):
        for c in range(tiles):
            index = rows_ref[p * tiles + c]
            group = lax.shift_right_logical(index, LANE_BITS)
            lane = index & (LANES - 1)
            found = [jnp.zeros((ROWS, LANES), jnp.float32)] * 3
            for g in range(groups):
                here = group == g
                for k in range(3):
                    value = jnp.take_along_axis(table_ref[p, g * 3 + k], lane, axis=1)
                    found[k] = jnp.where(here, value, found[k])
            for k in range(3):
                out_ref[k, p * tiles + c] = found[k]


def moment_slot(a, e):
    return a * len(SYM3) + e


def mixed_slot(a, c):
    return len(SYM4) * len(SYM3) + 4 * a + c


END_SLOT = mixed_slot(4, 0)
ANCHOR_SLOT = END_SLOT + 2
N_SLOTS = ANCHOR_SLOT + 1


def moment_body(
    target_ref,
    tile_ref,
    anchor_ref,
    points_ref,
    lane_ref,
    window_ref,
    out_ref,
    table_ref,
    rows_ref,
):
    scans, edges, tiles, _ = lane_ref.shape
    bnd = window_ref.shape[0] // (3 * scans * lax.axis_size("dom"))
    pack = ROWS // edges
    lane_groups = out_ref.shape[1]
    for s in range(scans):
        for j in range(edges):
            for c in range(tiles):
                at = (s // pack) * tiles + c
                if j == 0:
                    row = (s % pack) * edges
                    rows_ref[at, row : row + edges] = lane_ref[s, :, c, :]
                which = target_ref[s, j] * bnd + tile_ref[s, j, c]
                table_ref[at, :, (s % pack) * edges + j, :] = window_ref[which]
    place = lax.broadcasted_iota(jnp.int32, (ROWS, LANES), 1) - (
        lax.broadcasted_iota(jnp.int32, (ROWS, LANES), 0) % edges
    )
    lane_row = lax.broadcasted_iota(jnp.int32, (1, LANES), 1)
    scale = 1.0 / (tiles * LANES)
    lines = [[] for _ in range(lane_groups)]
    for p in range(scans // pack):
        gathered = [jnp.zeros((ROWS, LANES), jnp.float32) for _ in range(lane_groups)]
        sums = {}

        def collect(slot, value, sums=sums):
            sums[slot] = sums[slot] + value if slot in sums else value

        for c in range(tiles):
            at = p * tiles + c
            lanes = rows_ref[at]
            got = [jnp.take_along_axis(table_ref[at, k], lanes, axis=1) for k in range(4)]
            point = [points_ref[k, at] for k in range(3)]
            pairs = [got[a] * got[b] for a, b in SYM3]
            weighted = [got[a] * got[3] for a in range(3)]
            for q, (a, b) in enumerate(SYM4):
                if a == 3:
                    values = pairs
                else:
                    factor = point[a] if b == 3 else point[a] * point[b]
                    values = [factor * pair for pair in pairs]
                for e, value in enumerate(values):
                    collect(moment_slot(q, e), value)
            for a in range(4):
                for k in range(3):
                    value = weighted[k] if a == 3 else point[a] * weighted[k]
                    collect(mixed_slot(a, k), value)
        for slot, value in sums.items():
            total = jnp.sum(value, axis=1, keepdims=True)
            g, off = divmod(slot * edges, LANES)
            gathered[g] = jnp.where(place == off, total, gathered[g])
        for n in range(pack):
            s = p * pack + n
            flat = [
                jnp.sum(part[n * edges : (n + 1) * edges], axis=0, keepdims=True) * scale
                for part in gathered
            ]
            for j in range(2 * edges):
                g, off = divmod(END_SLOT * edges + j, LANES)
                slot = target_ref[s, j % edges].astype(jnp.float32)
                flat[g] = jnp.where(lane_row == off, slot, flat[g])
            g, off = divmod(ANCHOR_SLOT * edges, LANES)
            flat[g] = jnp.where(lane_row == off, anchor_ref[s], flat[g])
            for g in range(lane_groups):
                lines[g].append(flat[g])
    for g in range(lane_groups):
        block = jnp.concatenate(lines[g], axis=0)
        for d in range(out_ref.shape[0]):
            out_ref[d, g] = block


def sum_of(terms):
    total = None
    for term in terms:
        total = term if total is None else total + term
    return total


def product(left, right):
    return [
        [sum_of(left[a][k] * right[k][b] for k in range(3)) for b in range(3)] for a in range(3)
    ]


def transposed(matrix):
    return [[matrix[b][a] for b in range(3)] for a in range(3)]


def applied(matrix, vector):
    return [sum_of(matrix[a][k] * vector[k] for k in range(3)) for a in range(3)]


def cross(left, right):
    return [
        left[1] * right[2] - left[2] * right[1],
        left[2] * right[0] - left[0] * right[2],
        left[0] * right[1] - left[1] * right[0],
    ]


def rotated_sym(matrix, entries):
    half = product(matrix, [[entries[at3(m, k)] for k in range(3)] for m in range(3)])
    return [sum_of(half[a][k] * matrix[b][k] for k in range(3)) for a, b in SYM3]


NEXT = [(1, 2), (2, 0), (0, 1)]


def edge_terms(pair_of, own, far, swap):
    turn = [[far[3 * a + k] for k in range(3)] for a in range(3)]
    here = [[own[3 * a + k] for k in range(3)] for a in range(3)]
    start = own[9:12]
    back = transposed(turn)
    relative = product(back, here)
    shift = applied(back, [far[9 + a] - start[a] for a in range(3)])

    def halves(vector):
        return [vector, swap(vector)]

    mm = []
    xmm = [[] for _ in range(3)]
    xxmm = [[] for _ in range(6)]
    for e in range(0, len(SYM3), 2):
        moment = [pair_of(moment_slot(q, e)) for q in range(len(SYM4))]
        mm += halves(moment[at4(3, 3)])
        for a, part in enumerate(applied(relative, [moment[at4(k, 3)] for k in range(3)])):
            xmm[a] += halves(part)
        square = rotated_sym(relative, [moment[at4(a, b)] for a, b in SYM3])
        for n, part in enumerate(square):
            xxmm[n] += halves(part)
    mw = []
    xmw = [[] for _ in range(3)]
    for c in (0, 2):
        moment = [pair_of(mixed_slot(a, c)) for a in range(4)]
        mw += halves(moment[3])
        for a, part in enumerate(applied(relative, moment[:3])):
            xmw[a] += halves(part)

    def xm(a, c, d):
        return xmm[a][at3(c, d)]

    def xx(a, b, c, d):
        return xxmm[at3(a, b)][at3(c, d)]

    upper = []
    for i, i2 in SYM3:
        (j, k), (j2, k2) = NEXT[i], NEXT[i2]
        upper.append(xx(j, j2, k, k2) - xx(j, k2, k, j2) - xx(k, j2, j, k2) + xx(k, k2, j, j2))
    mixed = [[xm(j, k, d) - xm(k, j, d) for d in range(3)] for j, k in NEXT]
    lower = mm
    slope_upper = []
    for i, (j, k) in enumerate(NEXT):
        value = xmw[j][k] - xmw[k][j]
        value = value + sum_of(mixed[i][d] * shift[d] for d in range(3))
        slope_upper.append(value - sum_of(xx(j, d, k, d) - xx(k, d, j, d) for d in range(3)))
    slope_lower = []
    for i in range(3):
        value = mw[i] + sum_of(lower[at3(i, d)] * shift[d] for d in range(3))
        slope_lower.append(value - sum_of(xm(d, i, d) for d in range(3)))

    lower = rotated_sym(turn, lower)
    upper = rotated_sym(turn, upper)
    mixed = product(product(turn, mixed), back)
    slope_lower = applied(turn, slope_lower)
    slope_upper = applied(turn, slope_upper)
    slope_upper = [u + v for u, v in zip(slope_upper, cross(start, slope_lower))]
    turned = [cross(start, [lower[at3(k, d)] for k in range(3)]) for d in range(3)]
    moved_mixed = [[mixed[a][d] + turned[d][a] for d in range(3)] for a in range(3)]
    first = [cross(start, mixed[b]) for b in range(3)]
    second = [cross(start, moved_mixed[a]) for a in range(3)]
    block = [[None] * 6 for _ in range(6)]
    for n, (a, b) in enumerate(SYM3):
        block[a][b] = block[b][a] = upper[n] + first[b][a] + second[a][b]
        block[3 + a][3 + b] = block[3 + b][3 + a] = lower[n]
    for a in range(3):
        for d in range(3):
            block[a][3 + d] = block[3 + d][a] = moved_mixed[a][d]
    return block, slope_upper + slope_lower


def moved(pose, step):
    first, second, third = (0.5 * step[i] for i in range(3))
    length_sq = first * first + second * second + third * third
    inverse = 1.0 / (1.0 + length_sq)
    trace = 1.0 - length_sq
    turn = [
        [
            trace + 2.0 * first * first,
            2.0 * first * second - 2.0 * third,
            2.0 * first * third + 2.0 * second,
        ],
        [
            2.0 * first * second + 2.0 * third,
            trace + 2.0 * second * second,
            2.0 * second * third - 2.0 * first,
        ],
        [
            2.0 * first * third - 2.0 * second,
            2.0 * second * third + 2.0 * first,
            trace + 2.0 * third * third,
        ],
    ]
    turn = [[entry * inverse for entry in line] for line in turn]
    out = [
        sum_of(turn[a][k] * pose[3 * k + c] for k in range(3)) for a in range(3) for c in range(3)
    ]
    out += [sum_of(turn[a][k] * pose[9 + k] for k in range(3)) + step[3 + a] for a in range(3)]
    return out


def solve_body(first_ref, pose_ref, rows_ref, out_ref, moment_ref, *, edges, scan_sub):
    devices, lane_groups, scan_dev, _ = rows_ref.shape
    scans = devices * scan_dev
    chunks = scans // LANES
    half = ROWS // 2
    blocks = [rows_ref[:, g].reshape(scans, LANES) for g in range(lane_groups)]
    for g in range(lane_groups):
        moment_ref[g * LANES : (g + 1) * LANES] = blocks[g].T

    def pair_of(slot):
        return moment_ref[slot * edges : slot * edges + ROWS]

    def end_of(slots, scan):
        end = (scan // scan_sub) * scan_sub + slots - scan_sub
        end = jnp.where(end < 0, end + scans, end)
        return jnp.where(end >= scans, end - scans, end)

    end = end_of(
        pair_of(END_SLOT).astype(jnp.int32), lax.broadcasted_iota(jnp.int32, (ROWS, scans), 1)
    )
    anchor = moment_ref[ANCHOR_SLOT * edges : ANCHOR_SLOT * edges + 1]
    g, off = divmod(END_SLOT * edges, LANES)
    minus = []
    plus = []
    for j in range(edges):
        slots = blocks[g][:, off + j : off + j + 1].astype(jnp.int32)
        down = lax.broadcasted_iota(jnp.int32, (scans, scans), 0)
        far = end_of(slots, lax.broadcasted_iota(jnp.int32, (scans, 1), 0))
        across = lax.broadcasted_iota(jnp.int32, (scans, scans), 1)
        here = jnp.where(down == across, 1.0, 0.0)
        there = jnp.where(far == across, 1.0, 0.0)
        minus.append((here - there).astype(jnp.bfloat16))
        plus.append((here + there).astype(jnp.bfloat16))
    minus = jnp.concatenate(minus, axis=0)
    plus = jnp.concatenate(plus, axis=0)
    upper = lax.broadcasted_iota(jnp.int32, (ROWS, scans), 0) < edges

    def swap(vector):
        return jnp.concatenate([vector[half:], vector[:half]], axis=0)

    def wide(line):
        return jnp.broadcast_to(line, (ROWS, scans))

    def at_end(table):
        parts = []
        for o in range(chunks):
            index = end[:, o * LANES : (o + 1) * LANES]
            found = None
            for q in range(chunks):
                value = jnp.take_along_axis(
                    table[:, q * LANES : (q + 1) * LANES], index & (LANES - 1), axis=1
                )
                found = value if found is None else jnp.where(lax.shift_right_logical(index, LANE_BITS) == q, value, found)
            parts.append(found)
        return parts[0] if chunks == 1 else jnp.concatenate(parts, axis=1)

    def to_scans(planes, matrix):
        empty = jnp.zeros((ROWS - len(planes), scans), jnp.float32)
        full = jnp.concatenate(
            [
                jnp.concatenate([plane[j : j + 1] for plane in planes] + [empty], axis=0)
                for j in range(edges)
            ],
            axis=1,
        )
        high = full.astype(jnp.bfloat16).astype(jnp.float32)
        rest = full - high
        middle = rest.astype(jnp.bfloat16).astype(jnp.float32)
        pieces = jnp.concatenate([high, middle, rest - middle], axis=0).astype(jnp.bfloat16)
        out = jnp.dot(pieces, matrix, preferred_element_type=jnp.float32)
        return out[:ROWS] + out[ROWS : 2 * ROWS] + out[2 * ROWS :]

    def full_sum(value):
        return jnp.sum(jnp.sum(value, axis=1, keepdims=True), axis=0, keepdims=True)

    pose = [pose_ref[i : i + 1, :] for i in range(12)]
    for _ in range(GN_ITERS):
        own = [wide(line) for line in pose]
        block, slopes = edge_terms(pair_of, own, [at_end(line) for line in own], swap)
        residual = to_scans(slopes, minus)
        diagonal = to_scans([block[a][a] for a in range(6)], plus) + anchor

        def pushed_by(vector, block=block):
            lines = [wide(vector[a : a + 1]) for a in range(6)]
            spread = [line - at_end(line) for line in lines]
            return spread, [sum_of(block[a][b] * spread[b] for b in range(6)) for a in range(6)]

        scaled = residual / diagonal
        direction = scaled
        energy = full_sum(residual * scaled)
        increment = jnp.zeros_like(residual)
        spread, pushed = pushed_by(direction)
        for sweep in range(CG_ITERS):
            inner = jnp.where(upper, sum_of(spread[a] * pushed[a] for a in range(6)), 0.0)
            step = energy / full_sum(inner + anchor * direction * direction)
            increment = increment + step * direction
            if sweep + 1 < CG_ITERS:
                image = to_scans(pushed, minus) + anchor * direction
                residual = residual - step * image
                scaled = residual / diagonal
                renewed = full_sum(residual * scaled)
                fresh_spread, fresh_pushed = pushed_by(scaled)
                ratio = renewed / energy
                spread = [fresh_spread[a] + ratio * spread[a] for a in range(6)]
                pushed = [fresh_pushed[a] + ratio * pushed[a] for a in range(6)]
                direction = scaled + ratio * direction
                energy = renewed
        pose = moved(pose, [increment[a : a + 1] for a in range(6)])
    final = jnp.concatenate(pose, axis=0)
    lane_at = lax.broadcasted_iota(jnp.int32, final.shape, 1)
    out_at = lax.broadcasted_iota(jnp.int32, (12, scan_dev), 1)
    result = jnp.zeros((12, scan_dev), jnp.float32)
    for s in range(scan_dev):
        column = jnp.sum(
            jnp.where(lane_at == first_ref[0] + s, final, 0.0), axis=1, keepdims=True
        )
        result = jnp.where(out_at == s, column, result)
    out_ref[...] = result.T


def local(source_points, boundary, poses, anchor, edge_target, corr_tile, corr_source, corr_lane):
    scan_dev, bnd = boundary.shape[:2]
    edges, tiles = corr_tile.shape[1:]
    doms = lax.axis_size("dom")
    subs = lax.axis_size("sub")
    devices = subs * doms
    scan_sub = scan_dev * doms
    vectors = scan_dev * edges * tiles // ROWS
    lane_groups = -(-N_SLOTS * edges // LANES)

    packed = pl.pallas_call(
        pack_body,
        out_shape=pltpu.VMEM((scan_dev * bnd, 4, LANES), jnp.float32),
        in_specs=[vmem()],
        out_specs=vmem(),
        name="pack",
    )(boundary.transpose(0, 2, 1, 3))
    before = lax.ppermute(packed, "sub", [((i - 1) % subs, i) for i in range(subs)])
    beyond = lax.ppermute(packed, "sub", [((i + 1) % subs, i) for i in range(subs)])
    picked = pl.pallas_call(
        pick_body,
        out_shape=pltpu.VMEM((3, vectors, ROWS, LANES), jnp.float32),
        in_specs=[vmem(), vmem()],
        out_specs=vmem(),
        scratch_shapes=[
            pltpu.VMEM(
                (scan_dev * edges // ROWS, 3 * source_points.shape[2] // LANES, ROWS, LANES),
                jnp.float32,
            ),
            pltpu.VMEM((vectors, ROWS, LANES), jnp.int32),
        ],
        name="pick",
    )(source_points.transpose(1, 0, 2), corr_source)
    window = lax.all_gather(jnp.stack([before, packed, beyond]), "dom", axis=1, tiled=True)
    window = window.reshape(3 * scan_sub * bnd, 4, LANES)
    rows = pl.pallas_call(
        moment_body,
        out_shape=pltpu.VMEM((devices, lane_groups, scan_dev, LANES), jnp.float32),
        in_specs=[smem(), smem(), smem(), vmem(), vmem(), vmem()],
        out_specs=vmem(),
        scratch_shapes=[
            pltpu.VMEM((vectors, 4, ROWS, LANES), jnp.float32),
            pltpu.VMEM((vectors, ROWS, LANES), jnp.int32),
        ],
        name="moments",
    )(edge_target, corr_tile, anchor, in_vmem(picked), in_vmem(corr_lane), in_vmem(window))
    rows = lax.all_to_all(rows, AXES, 0, 0)
    first = (lax.axis_index(AXES) * scan_dev).astype(jnp.int32).reshape(1)
    return pl.pallas_call(
        functools.partial(solve_body, edges=edges, scan_sub=scan_sub),
        out_shape=jax.ShapeDtypeStruct((scan_dev, 12), jnp.float32),
        in_specs=[smem(), vmem(), vmem()],
        out_specs=vmem(),
        scratch_shapes=[
            pltpu.VMEM((lane_groups * LANES, devices * scan_dev), jnp.float32),
        ],
        name="solve",
    )(first, in_vmem(poses), in_vmem(rows)).T


def solution(mesh):
    in_specs = (
        P(AXES, None, None),
        P(AXES, None, None, None),
        P(),
        P(AXES),
        P(AXES, None),
        P(AXES, None, None),
        P(AXES, None, None, None),
        P(AXES, None, None, None),
    )
    out_specs = P(None, AXES)
    return jax.shard_map(local, mesh=mesh, in_specs=in_specs, out_specs=out_specs, check_vma=False)
```

time: 39.8 us -> 37 us (0.930)
  Pallas kernels: 10.1 us -> 7.29 us
    pallas_call x1, Pallas kernels: 4.27 us -> 2.45 us  [local(): pl.pallas_call(functools.partial(solve_body, edges=edges, scan_sub=scan_s...]
    pallas_call x1, Pallas kernels: 3.06 us -> 2.07 us  [local(): pl.pallas_call(moment_body, out_shape=pltpu.VMEM((devices, lane_groups, s...]
where the time goes in v3:
time: 37 us; the launch traced here: 36.7 us
  blocking collectives  10.1 us (27%)
  starting transfers between devices  9.98 us (27%)
  waiting for transfers between devices  9.19 us (25%)
  Pallas kernels  7.29 us (20%)
    all_gather x1, blocking collectives, local(): lax.all_gather(jnp.stack([before, packed, beyond]), 'dom', axis=1, tiled=...  10.1 us
    all_to_all x1, waiting for transfers between devices, local(): rows = lax.all_to_all(rows, AXES, 0, 0)  9.19 us
    all_to_all x1, starting transfers between devices, local(): rows = lax.all_to_all(rows, AXES, 0, 0)  4.76 us
    ppermute x1, starting transfers between devices, local(): lax.ppermute(packed, 'sub', [((i + 1) % subs, i) for i in range(subs)])  3.1 us
    pallas_call x1, Pallas kernels, local(): pl.pallas_call(functools.partial(solve_body, edges=edges, scan_sub=scan_s...  2.45 us
    ppermute x1, starting transfers between devices, local(): lax.ppermute(packed, 'sub', [((i - 1) % subs, i) for i in range(subs)])  2.11 us
    pallas_call x1, Pallas kernels, local(): pl.pallas_call(moment_body, out_shape=pltpu.VMEM((devices, lane_groups, s...  2.07 us
    pallas_call x1, Pallas kernels, local(): pl.pallas_call(pick_body, out_shape=pltpu.VMEM((3, vectors, ROWS, LANES),...  1.84 us
  transfers between devices with their start and end apart: 3, of which 1 were waited for; matrix products, arithmetic and copies ran while one was open for 0% of the time, Pallas kernels for 5%

profile of v3, /device:TPU:1, one launch (start us, length us, event | category | flops | bytes accessed | tf_op | source)
XLA Modules:
  0.0 36.7 jit_solution(2917872819469348182)
XLA Ops:
  0.0 0.9 %pack.1 = f32[32,4,128]{2,1,0:T(4,128)S(1)} custom-call(f32[4,6,8,128]{3,2,1,0:T(8,128)} %bitcast.11), custom_call_target="tpu_custom_call" | custom-call | tf_op jit(solution)/shard_map/pack/pallas_call | solution.py:446
  0.9 2.1 %collective-permute-start = (f32[32,4,128]{2,1,0:T(4,128)S(1)}, f32[32,4,128]{2,1,0:T(4,128)S(1)}, u32[]{:S(2)}, u32[]{:S(2)}) collective-permute-start(f32[32,4,128]{2,1,0:T(4,128)S(1)} %pack.1), channel_id=1, source_target_pairs={{28,0},{0,4},{4,8},{8,12},{12,16},{16,20},{20,24},{24,28},{29,1},{... | collective-permute-start | bytes 196616 | tf_op jit(solution)/shard_map/ppermute | solution.py:453
  3.0 3.1 %collective-permute-start.1 = (f32[32,4,128]{2,1,0:T(4,128)S(1)}, f32[32,4,128]{2,1,0:T(4,128)S(1)}, u32[]{:S(2)}, u32[]{:S(2)}) collective-permute-start(f32[32,4,128]{2,1,0:T(4,128)S(1)} %pack.1), channel_id=1, source_target_pairs={{4,0},{8,4},{12,8},{16,12},{20,16},{24,20},{28,24},{0,28},{5,1},{9... | collective-permute-start | bytes 196616 | tf_op jit(solution)/shard_map/ppermute | solution.py:454
  6.2 1.8 %pick.1.points_ref = f32[3,8,8,128]{3,2,1,0:T(8,128)S(1)} custom-call(f32[3,4,4096]{2,1,0:T(4,128)} %bitcast.10, s32[4,4,4,128]{3,2,1,0:T(4,128)} %index_ref.1), custom_call_target="tpu_custom_call" | custom-call | tf_op jit(solution)/shard_map/pick/pallas_call | solution.py:455
  8.0 0.0 collective-permute-done
  8.0 0.0 collective-permute-done.1
  8.1 0.0 copy-start
  8.1 10.1 %all_gather.3 = f32[3,128,4,128]{3,2,1,0:T(4,128)S(1)} all-gather(f32[3,32,4,128]{3,2,1,0:T(4,128)S(1)} %pad_maximum_fusion), channel_id=1, replica_groups=mesh['sub'=8,'dom'=4] {'dom'}, dimensions={1}, use_global_device_ids=true | all-gather | bytes 983040 | tf_op jit(solution)/shard_map/all_gather | solution.py:469
  18.2 0.0 copy-done
  18.2 2.1 %moments.1 = f32[32,3,4,128]{3,2,1,0:T(4,128)} custom-call(s32[4,4]{1,0:T(4,128)} %target_ref.1, s32[4,4,4]{2,1,0:T(4,128)} %tile_ref.1, f32[4]{0:T(128)} %anchor_ref.1, f32[3,8,8,128]{3,2,1,0:T(8,128)S(1)} %pick.1.points_ref, s32[4,4,4,128]{3,2,1,0:T(4,128)S(1)} %copy-done, f32[384,4,128]{2,1,0:T(4,128)S(1)} %bitcast.8), custom_call_target="tpu_custom_call" | custom-call | tf_op jit(solution)/shard_map/moments/pallas_call | solution.py:471
  20.2 4.8 %all-to-all-start = ((f32[32,3,4,128]{3,2,1,0:T(4,128)}), f32[32,3,4,128]{3,2,1,0:T(4,128)S(1)}, u32[]{:S(2)}, u32[]{:S(2)}) async-start(f32[32,3,4,128]{3,2,1,0:T(4,128)} %moments.1), calls=%async_computation | async-start | bytes 393216 | tf_op jit(solution)/shard_map/all_to_all | solution.py:482
  25.0 0.0 copy-start.1
  25.0 9.2 %all-to-all-done.rows_ref = f32[32,3,4,128]{3,2,1,0:T(4,128)S(1)} async-done(((f32[32,3,4,128]{3,2,1,0:T(4,128)}), f32[32,3,4,128]{3,2,1,0:T(4,128)S(1)}, u32[]{:S(2)}, u32[]{:S(2)}) %all-to-all-start) | async-done | bytes 196640 | tf_op jit(solution)/shard_map/all_to_all | solution.py:482
  34.2 0.0 copy-done.1
  34.2 2.5 %solve.1 = f32[4,12]{1,0:T(4,128)} custom-call(s32[1]{0:T(128)} %bitcast.first_ref, f32[12,128]{1,0:T(8,128)S(1)} %copy-done.1, f32[32,3,4,128]{3,2,1,0:T(4,128)S(1)} %all-to-all-done.rows_ref), custom_call_target="tpu_custom_call" | custom-call | tf_op jit(solution)/shard_map/solve/pallas_call | solution.py:484
  (1 shorter events, 0.0 us)
Async XLA Ops:
  0.9 7.1 %collective-permute-start = (f32[32,4,128]{2,1,0:T(4,128)S(1)}, f32[32,4,128]{2,1,0:T(4,128)S(1)}, u32[]{:S(2)}, u32[]{:S(2)}) collective-permute-start(f32[32,4,128]{2,1,0:T(4,128)S(1)} %pack.1), channel_id=1, source_target_pairs={{28,0},{0,4},{4,8},{8,12},{12,16},{16,20},{20,24},{24,28},{29,1},{... | collective-permute-start | bytes 196616 | tf_op jit(solution)/shard_map/ppermute | solution.py:453
  3.0 5.0 %collective-permute-start.1 = (f32[32,4,128]{2,1,0:T(4,128)S(1)}, f32[32,4,128]{2,1,0:T(4,128)S(1)}, u32[]{:S(2)}, u32[]{:S(2)}) collective-permute-start(f32[32,4,128]{2,1,0:T(4,128)S(1)} %pack.1), channel_id=1, source_target_pairs={{4,0},{8,4},{12,8},{16,12},{20,16},{24,20},{28,24},{0,28},{5,1},{9... | collective-permute-start | bytes 196616 | tf_op jit(solution)/shard_map/ppermute | solution.py:454
  8.1 10.1 %copy-start = (s32[4,4,4,128]{3,2,1,0:T(4,128)S(1)}, s32[4,4,4,128]{3,2,1,0:T(4,128)}, u32[]{:S(2)}) copy-start(s32[4,4,4,128]{3,2,1,0:T(4,128)} %lane_ref.1) | copy-start | bytes 98308
  20.2 14.0 %all-to-all-start = ((f32[32,3,4,128]{3,2,1,0:T(4,128)}), f32[32,3,4,128]{3,2,1,0:T(4,128)S(1)}, u32[]{:S(2)}, u32[]{:S(2)}) async-start(f32[32,3,4,128]{3,2,1,0:T(4,128)} %moments.1), calls=%async_computation | async-start | bytes 393216 | tf_op jit(solution)/shard_map/all_to_all | solution.py:482
  25.0 9.2 %copy-start.1 = (f32[12,128]{1,0:T(8,128)S(1)}, f32[12,128]{1,0:T(8,128)}, u32[]{:S(2)}) copy-start(f32[12,128]{1,0:T(8,128)} %pose_ref.1) | copy-start | bytes 18436

commit v4 on v3

--- a/solution.py
+++ b/solution.py
@@ -6,6 +6,7 @@
 from jax.experimental import pallas as pl
 from jax.experimental.pallas import tpu as pltpu
 from jax.sharding import PartitionSpec as P
+
 
 CG_ITERS = 2
 GN_ITERS = 2
@@ -47,15 +48,83 @@
             out_ref[s * bnd : (s + 1) * bnd, c, :] = part[3 + c]
 
 
-def pick_body(points_ref, index_ref, out_ref, table_ref, rows_ref):
+PIECES = [[0, 2, 1], [4, 6, 5], [8, 3, 9], [10, 7, 11]]
+
+
+def window_of(packed, subs, doms):
+    before = lax.ppermute(packed, "sub", [((i - 1) % subs, i) for i in range(subs)])
+    beyond = lax.ppermute(packed, "sub", [((i + 1) % subs, i) for i in range(subs)])
+    if doms != len(PIECES):
+        window = lax.all_gather(jnp.stack([before, packed, beyond]), "dom", axis=1, tiled=True)
+        return window.reshape(-1, *packed.shape[1:])
+
+    def partner(array, distance):
+        return lax.ppermute(array, "dom", [(i ^ distance, i) for i in range(doms)])
+
+    own = jnp.concatenate([before, beyond, packed, partner(packed, 2)], axis=0)
+    far = partner(own[: 2 * packed.shape[0]], 2)
+    near = partner(own, 1)
+    return jnp.concatenate([own, near, far, partner(far, 1)], axis=0)
+
+
+def place_of(target, scans, scan_sub):
+    if scan_sub // scans != len(PIECES):
+        return target
+    slot = lax.div(target, scan_sub)
+    inside = lax.rem(target, scan_sub)
+    apart = lax.div(inside, scans) ^ lax.axis_index("dom")
+    piece = jnp.int32(0)
+    for n, line in enumerate(PIECES):
+        for k, at in enumerate(line):
+            piece = jnp.where((apart == n) & (slot == k), jnp.int32(at), piece)
+    return piece * scans + lax.rem(inside, scans)
+
+
+def pick_body(
+    target_ref,
+    tile_ref,
+    anchor_ref,
+    points_ref,
+    index_ref,
+    lane_ref,
+    out_ref,
+    lanes_ref,
+    which_ref,
+    tail_ref,
+    table_ref,
+    rows_ref,
+    *,
+    bnd,
+):
     scans, edges, tiles, _ = index_ref.shape
     pack = ROWS // edges
     groups = points_ref.shape[2] // LANES
     row_at = lax.broadcasted_iota(jnp.int32, (ROWS, LANES), 0)
+    lane_row = lax.broadcasted_iota(jnp.int32, (1, LANES), 1)
+    subs = lax.axis_size("sub")
+    scan_sub = scans * lax.axis_size("dom")
     for s in range(scans):
+        tail = jnp.zeros((1, LANES), jnp.float32)
+        for j in range(edges):
+            target = target_ref[s, j]
+            group = lax.rem(lax.axis_index("sub") + lax.div(target, scan_sub) + subs - 1, subs)
+            end = (group * scan_sub + lax.rem(target, scan_sub)).astype(jnp.float32)
+            for at in (END_SLOT * edges + j, (END_SLOT + 1) * edges + j):
+                tail = jnp.where(lane_row == at % LANES, end, tail)
+            first = place_of(target, scans, scan_sub) * bnd
+            for c in range(tiles):
+                row = (s * edges + j) * tiles + c
+                which_ref[row : row + 1] = jnp.full(
+                    (1, LANES), first + tile_ref[s, j, c], jnp.int32
+                )
+        tail_ref[s : s + 1] = jnp.where(
+            lane_row == ANCHOR_SLOT * edges % LANES, anchor_ref[s], tail
+        )
         for c in range(tiles):
             at = (s // pack) * tiles + c
-            rows_ref[at, (s % pack) * edges : (s % pack + 1) * edges] = index_ref[s, :, c, :]
+            own = slice((s % pack) * edges, (s % pack + 1) * edges)
+            rows_ref[at, own] = index_ref[s, :, c, :]
+            lanes_ref[at, own] = lane_ref[s, :, c, :]
     for p in range(scans // pack):
         for g in range(groups):
             for k in range(3):
@@ -95,33 +164,19 @@
 
 
 def moment_body(
-    target_ref,
-    tile_ref,
-    anchor_ref,
-    points_ref,
-    lane_ref,
-    window_ref,
-    out_ref,
-    table_ref,
-    rows_ref,
+    which_ref, tail_ref, points_ref, lanes_ref, window_ref, out_ref, table_ref, *, edges, tiles
 ):
-    scans, edges, tiles, _ = lane_ref.shape
-    bnd = window_ref.shape[0] // (3 * scans * lax.axis_size("dom"))
+    lane_groups, scans = out_ref.shape[1:3]
     pack = ROWS // edges
-    lane_groups = out_ref.shape[1]
     for s in range(scans):
         for j in range(edges):
             for c in range(tiles):
+                which = which_ref[(s * edges + j) * tiles + c, 0]
                 at = (s // pack) * tiles + c
-                if j == 0:
-                    row = (s % pack) * edges
-                    rows_ref[at, row : row + edges] = lane_ref[s, :, c, :]
-                which = target_ref[s, j] * bnd + tile_ref[s, j, c]
                 table_ref[at, :, (s % pack) * edges + j, :] = window_ref[which]
     place = lax.broadcasted_iota(jnp.int32, (ROWS, LANES), 1) - (
         lax.broadcasted_iota(jnp.int32, (ROWS, LANES), 0) % edges
     )
-    lane_row = lax.broadcasted_iota(jnp.int32, (1, LANES), 1)
     scale = 1.0 / (tiles * LANES)
     lines = [[] for _ in range(lane_groups)]
     for p in range(scans // pack):
@@ -133,7 +188,7 @@
 
         for c in range(tiles):
             at = p * tiles + c
-            lanes = rows_ref[at]
+            lanes = lanes_ref[at]
             got = [jnp.take_along_axis(table_ref[at, k], lanes, axis=1) for k in range(4)]
             point = [points_ref[k, at] for k in range(3)]
             pairs = [got[a] * got[b] for a, b in SYM3]
@@ -160,16 +215,12 @@
                 jnp.sum(part[n * edges : (n + 1) * edges], axis=0, keepdims=True) * scale
                 for part in gathered
             ]
-            for j in range(2 * edges):
-                g, off = divmod(END_SLOT * edges + j, LANES)
-                slot = target_ref[s, j % edges].astype(jnp.float32)
-                flat[g] = jnp.where(lane_row == off, slot, flat[g])
-            g, off = divmod(ANCHOR_SLOT * edges, LANES)
-            flat[g] = jnp.where(lane_row == off, anchor_ref[s], flat[g])
             for g in range(lane_groups):
                 lines[g].append(flat[g])
     for g in range(lane_groups):
         block = jnp.concatenate(lines[g], axis=0)
+        if g == lane_groups - 1:
+            block = block + tail_ref[...]
         for d in range(out_ref.shape[0]):
             out_ref[d, g] = block
 
@@ -313,7 +364,7 @@
     return out
 
 
-def solve_body(first_ref, pose_ref, rows_ref, out_ref, moment_ref, *, edges, scan_sub):
+def solve_body(first_ref, pose_ref, rows_ref, out_ref, moment_ref, final_ref, *, edges):
     devices, lane_groups, scan_dev, _ = rows_ref.shape
     scans = devices * scan_dev
     chunks = scans // LANES
@@ -325,25 +376,17 @@
     def pair_of(slot):
         return moment_ref[slot * edges : slot * edges + ROWS]
 
-    def end_of(slots, scan):
-        end = (scan // scan_sub) * scan_sub + slots - scan_sub
-        end = jnp.where(end < 0, end + scans, end)
-        return jnp.where(end >= scans, end - scans, end)
-
-    end = end_of(
-        pair_of(END_SLOT).astype(jnp.int32), lax.broadcasted_iota(jnp.int32, (ROWS, scans), 1)
-    )
+    end = pair_of(END_SLOT).astype(jnp.int32)
     anchor = moment_ref[ANCHOR_SLOT * edges : ANCHOR_SLOT * edges + 1]
     g, off = divmod(END_SLOT * edges, LANES)
+    down = lax.broadcasted_iota(jnp.int32, (scans, scans), 0)
+    across = lax.broadcasted_iota(jnp.int32, (scans, scans), 1)
+    here = jnp.where(down == across, 1.0, 0.0)
+    across = across.astype(jnp.float32)
     minus = []
     plus = []
     for j in range(edges):
-        slots = blocks[g][:, off + j : off + j + 1].astype(jnp.int32)
-        down = lax.broadcasted_iota(jnp.int32, (scans, scans), 0)
-        far = end_of(slots, lax.broadcasted_iota(jnp.int32, (scans, 1), 0))
-        across = lax.broadcasted_iota(jnp.int32, (scans, scans), 1)
-        here = jnp.where(down == across, 1.0, 0.0)
-        there = jnp.where(far == across, 1.0, 0.0)
+        there = jnp.where(blocks[g][:, off + j : off + j + 1] == across, 1.0, 0.0)
         minus.append((here - there).astype(jnp.bfloat16))
         plus.append((here + there).astype(jnp.bfloat16))
     minus = jnp.concatenate(minus, axis=0)
@@ -421,25 +464,16 @@
                 direction = scaled + ratio * direction
                 energy = renewed
         pose = moved(pose, [increment[a : a + 1] for a in range(6)])
-    final = jnp.concatenate(pose, axis=0)
-    lane_at = lax.broadcasted_iota(jnp.int32, final.shape, 1)
-    out_at = lax.broadcasted_iota(jnp.int32, (12, scan_dev), 1)
-    result = jnp.zeros((12, scan_dev), jnp.float32)
-    for s in range(scan_dev):
-        column = jnp.sum(
-            jnp.where(lane_at == first_ref[0] + s, final, 0.0), axis=1, keepdims=True
-        )
-        result = jnp.where(out_at == s, column, result)
-    out_ref[...] = result.T
-
-
-def local(source_points, boundary, poses, anchor, edge_target, corr_tile, corr_source, corr_lane):
+    final_ref[...] = jnp.concatenate(pose, axis=0).T
+    out_ref[...] = final_ref[pl.ds(pl.multiple_of(first_ref[0], scan_dev), scan_dev)]
+
+
+def refined(source_points, boundary, poses, anchor, edge_target, corr_tile, corr_source, corr_lane):
     scan_dev, bnd = boundary.shape[:2]
     edges, tiles = corr_tile.shape[1:]
     doms = lax.axis_size("dom")
     subs = lax.axis_size("sub")
     devices = subs * doms
-    scan_sub = scan_dev * doms
     vectors = scan_dev * edges * tiles // ROWS
     lane_groups = -(-N_SLOTS * edges // LANES)
 
@@ -449,14 +483,19 @@
         in_specs=[vmem()],
         out_specs=vmem(),
         name="pack",
-    )(boundary.transpose(0, 2, 1, 3))
-    before = lax.ppermute(packed, "sub", [((i - 1) % subs, i) for i in range(subs)])
-    beyond = lax.ppermute(packed, "sub", [((i + 1) % subs, i) for i in range(subs)])
-    picked = pl.pallas_call(
-        pick_body,
-        out_shape=pltpu.VMEM((3, vectors, ROWS, LANES), jnp.float32),
-        in_specs=[vmem(), vmem()],
-        out_specs=vmem(),
+    )(in_vmem(boundary.transpose(0, 2, 1, 3)))
+    window = window_of(packed, subs, doms)
+    assert END_SLOT * edges // LANES == lane_groups - 1
+    picked, lanes, which, tail = pl.pallas_call(
+        functools.partial(pick_body, bnd=bnd),
+        out_shape=[
+            pltpu.VMEM((3, vectors, ROWS, LANES), jnp.float32),
+            pltpu.VMEM((vectors, ROWS, LANES), jnp.int32),
+            pltpu.VMEM((vectors * ROWS, LANES), jnp.int32),
+            pltpu.VMEM((scan_dev, LANES), jnp.float32),
+        ],
+        in_specs=[smem(), smem(), smem(), vmem(), vmem(), vmem()],
+        out_specs=[vmem()] * 4,
         scratch_shapes=[
             pltpu.VMEM(
                 (scan_dev * edges // ROWS, 3 * source_points.shape[2] // LANES, ROWS, LANES),
@@ -465,29 +504,32 @@
             pltpu.VMEM((vectors, ROWS, LANES), jnp.int32),
         ],
         name="pick",
-    )(source_points.transpose(1, 0, 2), corr_source)
-    window = lax.all_gather(jnp.stack([before, packed, beyond]), "dom", axis=1, tiled=True)
-    window = window.reshape(3 * scan_sub * bnd, 4, LANES)
+    )(
+        edge_target,
+        corr_tile,
+        anchor,
+        source_points.transpose(1, 0, 2),
+        corr_source,
+        corr_lane,
+    )
     rows = pl.pallas_call(
-        moment_body,
-        out_shape=pltpu.VMEM((devices, lane_groups, scan_dev, LANES), jnp.float32),
-        in_specs=[smem(), smem(), smem(), vmem(), vmem(), vmem()],
+        functools.partial(moment_body, edges=edges, tiles=tiles),
+        out_shape=jax.ShapeDtypeStruct((devices, lane_groups, scan_dev, LANES), jnp.float32),
+        in_specs=[vmem()] * 5,
         out_specs=vmem(),
-        scratch_shapes=[
-            pltpu.VMEM((vectors, 4, ROWS, LANES), jnp.float32),
-            pltpu.VMEM((vectors, ROWS, LANES), jnp.int32),
-        ],
+        scratch_shapes=[pltpu.VMEM((vectors, 4, ROWS, LANES), jnp.float32)],
         name="moments",
-    )(edge_target, corr_tile, anchor, in_vmem(picked), in_vmem(corr_lane), in_vmem(window))
+    )(*(in_vmem(array) for array in [which, tail, picked, lanes, window]))
     rows = lax.all_to_all(rows, AXES, 0, 0)
     first = (lax.axis_index(AXES) * scan_dev).astype(jnp.int32).reshape(1)
     return pl.pallas_call(
-        functools.partial(solve_body, edges=edges, scan_sub=scan_sub),
+        functools.partial(solve_body, edges=edges),
         out_shape=jax.ShapeDtypeStruct((scan_dev, 12), jnp.float32),
         in_specs=[smem(), vmem(), vmem()],
         out_specs=vmem(),
         scratch_shapes=[
             pltpu.VMEM((lane_groups * LANES, devices * scan_dev), jnp.float32),
+            pltpu.VMEM((devices * scan_dev, 12), jnp.float32),
         ],
         name="solve",
     )(first, in_vmem(poses), in_vmem(rows)).T
@@ -505,4 +547,7 @@
         P(AXES, None, None, None),
     )
     out_specs = P(None, AXES)
-    return jax.shard_map(local, mesh=mesh, in_specs=in_specs, out_specs=out_specs, check_vma=False)
+    step = jax.shard_map(refined, mesh=mesh, in_specs=in_specs, out_specs=out_specs, check_vma=False)
+    if mesh.shape["dom"] != len(PIECES):
+        return step
+    return step

time: 37 us -> 35.8 us (0.968)
  blocking collectives: 10.1 us -> 0 us
  starting transfers between devices: 9.98 us -> 15 us
  waiting for transfers between devices: 9.19 us -> 13.8 us
  Pallas kernels: 7.29 us -> 5.63 us
  local copies, waits for them, and re-layouts: 0.01 us -> 1.02 us
    all_gather x1 -> x0, blocking collectives: 10.1 us -> none  [local(): lax.all_gather(jnp.stack([before, packed, beyond]), 'dom', axis=1, tiled=...]
    ppermute x2 -> x6, starting transfers between devices: 5.21 us -> 10.8 us  [the longest x4 5.59 us: partner(): return lax.ppermute(array, 'dom', [(i ^ distance, i) for i in range(doms)])]
    ppermute x2 -> x6, waiting for transfers between devices: 0.01 us -> 4.59 us  [the longest x4 4.59 us: partner(): return lax.ppermute(array, 'dom', [(i ^ distance, i) for i in range(doms)])]
    pallas_call x4, Pallas kernels: 7.29 us -> 5.63 us  [the longest x1 2.43 us: refined(): pl.pallas_call(functools.partial(solve_body, edges=edges), out_shape=jax....]
    unnamed x4 -> x10, local copies, waits for them, and re-layouts: 0.01 us -> 1 us
    all_to_all x1, starting transfers between devices: 4.76 us -> 4.19 us  [refined(): rows = lax.all_to_all(rows, AXES, 0, 0)]
  transfers between devices with their start and end apart: 3 -> 7, of which waited for: 1 -> 3; matrix products, arithmetic and copies ran while one was open for 0% -> 0% of each run, Pallas kernels for 5% -> 5%
where the time goes in v4:
time: 35.8 us; the launch traced here: 35.6 us
  starting transfers between devices  15 us (42%)
  waiting for transfers between devices  13.8 us (39%)
  Pallas kernels  5.63 us (16%)
  local copies, waits for them, and re-layouts  1.02 us (3%)
    all_to_all x1, waiting for transfers between devices, refined(): rows = lax.all_to_all(rows, AXES, 0, 0)  9.19 us
    ppermute x4, starting transfers between devices, partner(): return lax.ppermute(array, 'dom', [(i ^ distance, i) for i in range(doms)])  5.59 us
    ppermute x4, waiting for transfers between devices, partner(): return lax.ppermute(array, 'dom', [(i ^ distance, i) for i in range(doms)])  4.59 us
    all_to_all x1, starting transfers between devices, refined(): rows = lax.all_to_all(rows, AXES, 0, 0)  4.19 us
    ppermute x1, starting transfers between devices, window_of(): lax.ppermute(packed, 'sub', [((i + 1) % subs, i) for i in range(subs)])  3.1 us
    pallas_call x1, Pallas kernels, refined(): pl.pallas_call(functools.partial(solve_body, edges=edges), out_shape=jax....  2.43 us
    ppermute x1, starting transfers between devices, window_of(): lax.ppermute(packed, 'sub', [((i - 1) % subs, i) for i in range(subs)])  2.11 us
    pallas_call x1, Pallas kernels, refined(): pl.pallas_call(functools.partial(pick_body, bnd=bnd), out_shape=[pltpu.VM...  1.9 us
  transfers between devices with their start and end apart: 7, of which 3 were waited for; matrix products, arithmetic and copies ran while one was open for 0% of the time, Pallas kernels for 5%

profile of v4, /device:TPU:1, one launch (start us, length us, event | category | flops | bytes accessed | tf_op | source)
XLA Modules:
  0.0 35.6 jit_solution(14530767890010441306)
XLA Ops:
  0.0 0.0 copy-start
  0.0 0.9 %copy-done = f32[4,8,6,128]{3,1,2,0:T(8,128)S(1)} copy-done((f32[4,8,6,128]{3,1,2,0:T(8,128)S(1)}, f32[4,8,6,128]{3,1,2,0:T(8,128)}, u32[]{:S(2)}) %copy-start) | copy-done | bytes 98328
  0.9 2.1 %collective-permute-start = (f32[32,4,128]{2,1,0:T(4,128)S(1)}, f32[32,4,128]{2,1,0:T(4,128)S(1)}, u32[]{:S(2)}, u32[]{:S(2)}) collective-permute-start(f32[32,4,128]{2,1,0:T(4,128)S(1)} %pack.1), channel_id=1, source_target_pairs={{28,0},{0,4},{4,8},{8,12},{12,16},{16,20},{20,24},{24,28},{29,1},{... | collective-permute-start | bytes 196616 | tf_op jit(solution)/shard_map/ppermute | solution.py:55
  3.0 3.1 %collective-permute-start.1 = (f32[32,4,128]{2,1,0:T(4,128)S(1)}, f32[32,4,128]{2,1,0:T(4,128)S(1)}, u32[]{:S(2)}, u32[]{:S(2)}) collective-permute-start(f32[32,4,128]{2,1,0:T(4,128)S(1)} %pack.1), channel_id=1, source_target_pairs={{4,0},{8,4},{12,8},{16,12},{20,16},{24,20},{28,24},{0,28},{5,1},{9... | collective-permute-start | bytes 196616 | tf_op jit(solution)/shard_map/ppermute | solution.py:56
  6.2 1.2 %collective-permute-start.2 = (f32[32,4,128]{2,1,0:T(4,128)S(1)}, f32[32,4,128]{2,1,0:T(4,128)S(1)}, u32[]{:S(2)}, u32[]{:S(2)}) collective-permute-start(f32[32,4,128]{2,1,0:T(4,128)S(1)} %pack.1), channel_id=1, source_target_pairs={{2,0},{3,1},{0,2},{1,3},{6,4},{7,5},{4,6},{5,7},{10,8},{11,9},{8,1... | collective-permute-start | bytes 196616 | tf_op jit(solution)/shard_map/ppermute | solution.py:62
  7.4 1.9 %pick.1 = (f32[3,8,8,128]{3,2,1,0:T(8,128)S(1)}, s32[8,8,128]{2,1,0:T(8,128)S(1)}, s32[64,128]{1,0:T(8,128)S(1)}, f32[4,128]{1,0:T(4,128)S(1)}) custom-call(s32[4,4]{1,0:T(4,128)} %target_ref.1, s32[4,4,4]{2,1,0:T(4,128)} %tile_ref.1, f32[4]{0:T(128)} %anchor_ref.1, f32[3,4,4096]{2,1,0:T(4,128)} %bitcast.5, s32[4,4,4,128]{3,2,1,0:T(4,128)} %index_ref.1, ...), custom_call_target="tpu_custom_call" | custom-call | tf_op jit(solution)/shard_map/pick/pallas_call | solution.py:489
  9.3 0.0 collective-permute-done
  9.3 0.0 collective-permute-done.1
  9.3 0.0 collective-permute-done.2
  9.3 0.1 pad_maximum_fusion
  9.4 2.1 %collective-permute-start.3 = (f32[128,4,128]{2,1,0:T(4,128)S(1)}, f32[128,4,128]{2,1,0:T(4,128)S(1)}, u32[]{:S(2)}, u32[]{:S(2)}) collective-permute-start(f32[128,4,128]{2,1,0:T(4,128)S(1)} %pad_maximum_fusion), channel_id=1, source_target_pairs={{1,0},{0,1},{3,2},{2,3},{5,4},{4,5},{7,6},{6,7},{9,8},{8,9},{11,10... | collective-permute-start | bytes 786440 | tf_op jit(solution)/shard_map/ppermute | solution.py:62
  11.5 1.4 %collective-permute-start.4 = (f32[64,4,128]{2,1,0:T(4,128)S(1)}, f32[64,4,128]{2,1,0:T(4,128)S(1)}, u32[]{:S(2)}, u32[]{:S(2)}) collective-permute-start(f32[64,4,128]{2,1,0:T(4,128)S(1)} %pad_maximum_fusion.1), channel_id=1, source_target_pairs={{2,0},{3,1},{0,2},{1,3},{6,4},{7,5},{4,6},{5,7},{10,8},{11,9},{8,1... | collective-permute-start | bytes 393224 | tf_op jit(solution)/shard_map/ppermute | solution.py:62
  13.0 3.7 %collective-permute-done.4 = f32[64,4,128]{2,1,0:T(4,128)S(1)} collective-permute-done((f32[64,4,128]{2,1,0:T(4,128)S(1)}, f32[64,4,128]{2,1,0:T(4,128)S(1)}, u32[]{:S(2)}, u32[]{:S(2)}) %collective-permute-start.4) | collective-permute-done | bytes 131104 | tf_op jit(solution)/shard_map/ppermute | solution.py:62
  16.6 0.9 %collective-permute-start.5 = (f32[64,4,128]{2,1,0:T(4,128)S(1)}, f32[64,4,128]{2,1,0:T(4,128)S(1)}, u32[]{:S(2)}, u32[]{:S(2)}) collective-permute-start(f32[64,4,128]{2,1,0:T(4,128)S(1)} %collective-permute-done.4), channel_id=1, source_target_pairs={{1,0},{0,1},{3,2},{2,3},{5,4},{4,5},{7,6},{6,7},{9,8},{8,9},{11,10... | collective-permute-start | bytes 393224 | tf_op jit(solution)/shard_map/ppermute | solution.py:62
  17.5 0.0 collective-permute-done.3
  17.6 0.9 %collective-permute-done.5 = f32[64,4,128]{2,1,0:T(4,128)S(1)} collective-permute-done((f32[64,4,128]{2,1,0:T(4,128)S(1)}, f32[64,4,128]{2,1,0:T(4,128)S(1)}, u32[]{:S(2)}, u32[]{:S(2)}) %collective-permute-start.5) | collective-permute-done | bytes 131104 | tf_op jit(solution)/shard_map/ppermute | solution.py:62
  18.5 1.3 %moments.1 = f32[32,3,4,128]{3,2,1,0:T(4,128)} custom-call(s32[64,128]{1,0:T(8,128)S(1)} %get-tuple-element.9.which_ref, f32[4,128]{1,0:T(4,128)S(1)} %get-tuple-element.10.tail_ref, f32[3,8,8,128]{3,2,1,0:T(8,128)S(1)} %get-tuple-element.11.points_ref, s32[8,8,128]{2,1,0:T(8,128)S(1)} %get-tuple-element.12.lanes_ref, ...), custom_call_target="tpu_custom_call" | custom-call | tf_op jit(solution)/shard_map/moments/pallas_call | solution.py:515
  19.8 4.2 %all-to-all-start = ((f32[32,3,4,128]{3,2,1,0:T(4,128)}), f32[32,3,4,128]{3,2,1,0:T(4,128)S(1)}, u32[]{:S(2)}, u32[]{:S(2)}) async-start(f32[32,3,4,128]{3,2,1,0:T(4,128)} %moments.1), calls=%async_computation | async-start | bytes 393216 | tf_op jit(solution)/shard_map/all_to_all | solution.py:523
  24.0 0.0 copy-start.1
  24.0 9.2 %all-to-all-done.rows_ref = f32[32,3,4,128]{3,2,1,0:T(4,128)S(1)} async-done(((f32[32,3,4,128]{3,2,1,0:T(4,128)}), f32[32,3,4,128]{3,2,1,0:T(4,128)S(1)}, u32[]{:S(2)}, u32[]{:S(2)}) %all-to-all-start) | async-done | bytes 196640 | tf_op jit(solution)/shard_map/all_to_all | solution.py:523
  33.2 0.0 copy-done.1
  33.2 2.4 %solve.1 = f32[4,12]{1,0:T(4,128)} custom-call(s32[1]{0:T(128)} %bitcast.first_ref, f32[12,128]{1,0:T(8,128)S(1)} %copy-done.1, f32[32,3,4,128]{3,2,1,0:T(4,128)S(1)} %all-to-all-done.rows_ref), custom_call_target="tpu_custom_call" | custom-call | tf_op jit(solution)/shard_map/solve/pallas_call | solution.py:525
  (9 shorter events, 0.2 us)
Async XLA Ops:
  0.0 0.9 %copy-start = (f32[4,8,6,128]{3,1,2,0:T(8,128)S(1)}, f32[4,8,6,128]{3,1,2,0:T(8,128)}, u32[]{:S(2)}) copy-start(f32[4,8,6,128]{3,1,2,0:T(8,128)} %param.9) | copy-start | bytes 294916
  0.9 8.3 %collective-permute-start = (f32[32,4,128]{2,1,0:T(4,128)S(1)}, f32[32,4,128]{2,1,0:T(4,128)S(1)}, u32[]{:S(2)}, u32[]{:S(2)}) collective-permute-start(f32[32,4,128]{2,1,0:T(4,128)S(1)} %pack.1), channel_id=1, source_target_pairs={{28,0},{0,4},{4,8},{8,12},{12,16},{16,20},{20,24},{24,28},{29,1},{... | collective-permute-start | bytes 196616 | tf_op jit(solution)/shard_map/ppermute | solution.py:55
  3.0 6.2 %collective-permute-start.1 = (f32[32,4,128]{2,1,0:T(4,128)S(1)}, f32[32,4,128]{2,1,0:T(4,128)S(1)}, u32[]{:S(2)}, u32[]{:S(2)}) collective-permute-start(f32[32,4,128]{2,1,0:T(4,128)S(1)} %pack.1), channel_id=1, source_target_pairs={{4,0},{8,4},{12,8},{16,12},{20,16},{24,20},{28,24},{0,28},{5,1},{9... | collective-permute-start | bytes 196616 | tf_op jit(solution)/shard_map/ppermute | solution.py:56
  6.2 3.1 %collective-permute-start.2 = (f32[32,4,128]{2,1,0:T(4,128)S(1)}, f32[32,4,128]{2,1,0:T(4,128)S(1)}, u32[]{:S(2)}, u32[]{:S(2)}) collective-permute-start(f32[32,4,128]{2,1,0:T(4,128)S(1)} %pack.1), channel_id=1, source_target_pairs={{2,0},{3,1},{0,2},{1,3},{6,4},{7,5},{4,6},{5,7},{10,8},{11,9},{8,1... | collective-permute-start | bytes 196616 | tf_op jit(solution)/shard_map/ppermute | solution.py:62
  9.4 8.1 %collective-permute-start.3 = (f32[128,4,128]{2,1,0:T(4,128)S(1)}, f32[128,4,128]{2,1,0:T(4,128)S(1)}, u32[]{:S(2)}, u32[]{:S(2)}) collective-permute-start(f32[128,4,128]{2,1,0:T(4,128)S(1)} %pad_maximum_fusion), channel_id=1, source_target_pairs={{1,0},{0,1},{3,2},{2,3},{5,4},{4,5},{7,6},{6,7},{9,8},{8,9},{11,10... | collective-permute-start | bytes 786440 | tf_op jit(solution)/shard_map/ppermute | solution.py:62
  11.5 5.1 %collective-permute-start.4 = (f32[64,4,128]{2,1,0:T(4,128)S(1)}, f32[64,4,128]{2,1,0:T(4,128)S(1)}, u32[]{:S(2)}, u32[]{:S(2)}) collective-permute-start(f32[64,4,128]{2,1,0:T(4,128)S(1)} %pad_maximum_fusion.1), channel_id=1, source_target_pairs={{2,0},{3,1},{0,2},{1,3},{6,4},{7,5},{4,6},{5,7},{10,8},{11,9},{8,1... | collective-permute-start | bytes 393224 | tf_op jit(solution)/shard_map/ppermute | solution.py:62
  16.6 1.9 %collective-permute-start.5 = (f32[64,4,128]{2,1,0:T(4,128)S(1)}, f32[64,4,128]{2,1,0:T(4,128)S(1)}, u32[]{:S(2)}, u32[]{:S(2)}) collective-permute-start(f32[64,4,128]{2,1,0:T(4,128)S(1)} %collective-permute-done.4), channel_id=1, source_target_pairs={{1,0},{0,1},{3,2},{2,3},{5,4},{4,5},{7,6},{6,7},{9,8},{8,9},{11,10... | collective-permute-start | bytes 393224 | tf_op jit(solution)/shard_map/ppermute | solution.py:62
  19.8 13.4 %all-to-all-start = ((f32[32,3,4,128]{3,2,1,0:T(4,128)}), f32[32,3,4,128]{3,2,1,0:T(4,128)S(1)}, u32[]{:S(2)}, u32[]{:S(2)}) async-start(f32[32,3,4,128]{3,2,1,0:T(4,128)} %moments.1), calls=%async_computation | async-start | bytes 393216 | tf_op jit(solution)/shard_map/all_to_all | solution.py:523
  24.0 9.2 %copy-start.1 = (f32[12,128]{1,0:T(8,128)S(1)}, f32[12,128]{1,0:T(8,128)}, u32[]{:S(2)}) copy-start(f32[12,128]{1,0:T(8,128)} %pose_ref.1) | copy-start | bytes 18436

commit v5 on v4

--- a/solution.py
+++ b/solution.py
@@ -62,9 +62,12 @@
         return lax.ppermute(array, "dom", [(i ^ distance, i) for i in range(doms)])
 
     own = jnp.concatenate([before, beyond, packed, partner(packed, 2)], axis=0)
-    far = partner(own[: 2 * packed.shape[0]], 2)
+    far_before = partner(before, 2)
+    far_beyond = partner(beyond, 2)
+    far = jnp.concatenate([far_before, far_beyond], axis=0)
     near = partner(own, 1)
-    return jnp.concatenate([own, near, far, partner(far, 1)], axis=0)
+    last = partner(far, 1)
+    return jnp.concatenate([own, near, far, last], axis=0)
 
 
 def place_of(target, scans, scan_sub):

time: 35.8 us -> 36 us (level)
  starting transfers between devices: 15 us -> 15.4 us
    ppermute x4 -> x5, starting transfers between devices: 5.59 us -> 6.01 us  [partner(): return lax.ppermute(array, 'dom', [(i ^ distance, i) for i in range(doms)])]
    ppermute x4 -> x5, waiting for transfers between devices: 4.59 us -> 4.27 us  [partner(): return lax.ppermute(array, 'dom', [(i ^ distance, i) for i in range(doms)])]
    unnamed x10 -> x11, local copies, waits for them, and re-layouts: 1 us -> 1.01 us
  transfers between devices with their start and end apart: 7 -> 8, of which waited for: 3 -> 4; matrix products, arithmetic and copies ran while one was open for 0% -> 0% of each run, Pallas kernels for 5% -> 5%
where the time goes in v5:
time: 36 us; the launch traced here: 35.7 us
  starting transfers between devices  15.4 us (43%)
  waiting for transfers between devices  13.5 us (38%)
  Pallas kernels  5.64 us (16%)
  local copies, waits for them, and re-layouts  1.02 us (3%)
    all_to_all x1, waiting for transfers between devices, refined(): rows = lax.all_to_all(rows, AXES, 0, 0)  9.19 us
    ppermute x5, starting transfers between devices, partner(): return lax.ppermute(array, 'dom', [(i ^ distance, i) for i in range(doms)])  6.01 us
    ppermute x5, waiting for transfers between devices, partner(): return lax.ppermute(array, 'dom', [(i ^ distance, i) for i in range(doms)])  4.27 us
    all_to_all x1, starting transfers between devices, refined(): rows = lax.all_to_all(rows, AXES, 0, 0)  4.19 us
    ppermute x1, starting transfers between devices, window_of(): lax.ppermute(packed, 'sub', [((i + 1) % subs, i) for i in range(subs)])  3.1 us
    pallas_call x1, Pallas kernels, refined(): pl.pallas_call(functools.partial(solve_body, edges=edges), out_shape=jax....  2.43 us
    ppermute x1, starting transfers between devices, window_of(): lax.ppermute(packed, 'sub', [((i - 1) % subs, i) for i in range(subs)])  2.11 us
    pallas_call x1, Pallas kernels, refined(): pl.pallas_call(functools.partial(pick_body, bnd=bnd), out_shape=[pltpu.VM...  1.9 us
  transfers between devices with their start and end apart: 8, of which 4 were waited for; matrix products, arithmetic and copies ran while one was open for 0% of the time, Pallas kernels for 5%

profile of v5, /device:TPU:1, one launch (start us, length us, event | category | flops | bytes accessed | tf_op | source)
XLA Modules:
  0.0 35.7 jit_solution(4489259348611349508)
XLA Ops:
  0.0 0.0 copy-start
  0.0 0.9 %copy-done = f32[4,8,6,128]{3,1,2,0:T(8,128)S(1)} copy-done((f32[4,8,6,128]{3,1,2,0:T(8,128)S(1)}, f32[4,8,6,128]{3,1,2,0:T(8,128)}, u32[]{:S(2)}) %copy-start) | copy-done | bytes 98328
  0.9 2.1 %collective-permute-start = (f32[32,4,128]{2,1,0:T(4,128)S(1)}, f32[32,4,128]{2,1,0:T(4,128)S(1)}, u32[]{:S(2)}, u32[]{:S(2)}) collective-permute-start(f32[32,4,128]{2,1,0:T(4,128)S(1)} %pack.1), channel_id=1, source_target_pairs={{28,0},{0,4},{4,8},{8,12},{12,16},{16,20},{20,24},{24,28},{29,1},{... | collective-permute-start | bytes 196616 | tf_op jit(solution)/shard_map/ppermute | solution.py:55
  3.0 3.1 %collective-permute-start.1 = (f32[32,4,128]{2,1,0:T(4,128)S(1)}, f32[32,4,128]{2,1,0:T(4,128)S(1)}, u32[]{:S(2)}, u32[]{:S(2)}) collective-permute-start(f32[32,4,128]{2,1,0:T(4,128)S(1)} %pack.1), channel_id=1, source_target_pairs={{4,0},{8,4},{12,8},{16,12},{20,16},{24,20},{28,24},{0,28},{5,1},{9... | collective-permute-start | bytes 196616 | tf_op jit(solution)/shard_map/ppermute | solution.py:56
  6.2 1.2 %collective-permute-start.2 = (f32[32,4,128]{2,1,0:T(4,128)S(1)}, f32[32,4,128]{2,1,0:T(4,128)S(1)}, u32[]{:S(2)}, u32[]{:S(2)}) collective-permute-start(f32[32,4,128]{2,1,0:T(4,128)S(1)} %pack.1), channel_id=1, source_target_pairs={{2,0},{3,1},{0,2},{1,3},{6,4},{7,5},{4,6},{5,7},{10,8},{11,9},{8,1... | collective-permute-start | bytes 196616 | tf_op jit(solution)/shard_map/ppermute | solution.py:62
  7.4 1.9 %pick.1 = (f32[3,8,8,128]{3,2,1,0:T(8,128)S(1)}, s32[8,8,128]{2,1,0:T(8,128)S(1)}, s32[64,128]{1,0:T(8,128)S(1)}, f32[4,128]{1,0:T(4,128)S(1)}) custom-call(s32[4,4]{1,0:T(4,128)} %target_ref.1, s32[4,4,4]{2,1,0:T(4,128)} %tile_ref.1, f32[4]{0:T(128)} %anchor_ref.1, f32[3,4,4096]{2,1,0:T(4,128)} %bitcast.5, s32[4,4,4,128]{3,2,1,0:T(4,128)} %index_ref.1, ...), custom_call_target="tpu_custom_call" | custom-call | tf_op jit(solution)/shard_map/pick/pallas_call | solution.py:492
  9.3 0.0 collective-permute-done
  9.3 0.0 collective-permute-done.1
  9.3 0.0 collective-permute-done.2
  9.3 0.1 pad_maximum_fusion
  9.4 2.1 %collective-permute-start.3 = (f32[128,4,128]{2,1,0:T(4,128)S(1)}, f32[128,4,128]{2,1,0:T(4,128)S(1)}, u32[]{:S(2)}, u32[]{:S(2)}) collective-permute-start(f32[128,4,128]{2,1,0:T(4,128)S(1)} %pad_maximum_fusion), channel_id=1, source_target_pairs={{1,0},{0,1},{3,2},{2,3},{5,4},{4,5},{7,6},{6,7},{9,8},{8,9},{11,10... | collective-permute-start | bytes 786440 | tf_op jit(solution)/shard_map/ppermute | solution.py:62
  11.5 1.4 %collective-permute-start.4 = (f32[32,4,128]{2,1,0:T(4,128)S(1)}, f32[32,4,128]{2,1,0:T(4,128)S(1)}, u32[]{:S(2)}, u32[]{:S(2)}) collective-permute-start(f32[32,4,128]{2,1,0:T(4,128)S(1)} %collective-permute-done), channel_id=1, source_target_pairs={{2,0},{3,1},{0,2},{1,3},{6,4},{7,5},{4,6},{5,7},{10,8},{11,9},{8,1... | collective-permute-start | bytes 196616 | tf_op jit(solution)/shard_map/ppermute | solution.py:62
  12.9 0.2 collective-permute-start.5
  13.1 2.1 %collective-permute-done.4 = f32[32,4,128]{2,1,0:T(4,128)S(1)} collective-permute-done((f32[32,4,128]{2,1,0:T(4,128)S(1)}, f32[32,4,128]{2,1,0:T(4,128)S(1)}, u32[]{:S(2)}, u32[]{:S(2)}) %collective-permute-start.4) | collective-permute-done | bytes 65568 | tf_op jit(solution)/shard_map/ppermute | solution.py:62
  15.2 1.2 %collective-permute-done.5 = f32[32,4,128]{2,1,0:T(4,128)S(1)} collective-permute-done((f32[32,4,128]{2,1,0:T(4,128)S(1)}, f32[32,4,128]{2,1,0:T(4,128)S(1)}, u32[]{:S(2)}, u32[]{:S(2)}) %collective-permute-start.5) | collective-permute-done | bytes 65568 | tf_op jit(solution)/shard_map/ppermute | solution.py:62
  16.5 1.1 %collective-permute-start.6 = (f32[64,4,128]{2,1,0:T(4,128)S(1)}, f32[64,4,128]{2,1,0:T(4,128)S(1)}, u32[]{:S(2)}, u32[]{:S(2)}) collective-permute-start(f32[64,4,128]{2,1,0:T(4,128)S(1)} %pad_maximum_fusion.1), channel_id=1, source_target_pairs={{1,0},{0,1},{3,2},{2,3},{5,4},{4,5},{7,6},{6,7},{9,8},{8,9},{11,10... | collective-permute-start | bytes 393224 | tf_op jit(solution)/shard_map/ppermute | solution.py:62
  17.6 0.0 collective-permute-done.3
  17.7 0.9 %collective-permute-done.6 = f32[64,4,128]{2,1,0:T(4,128)S(1)} collective-permute-done((f32[64,4,128]{2,1,0:T(4,128)S(1)}, f32[64,4,128]{2,1,0:T(4,128)S(1)}, u32[]{:S(2)}, u32[]{:S(2)}) %collective-permute-start.6) | collective-permute-done | bytes 131104 | tf_op jit(solution)/shard_map/ppermute | solution.py:62
  18.6 1.3 %moments.1 = f32[32,3,4,128]{3,2,1,0:T(4,128)} custom-call(s32[64,128]{1,0:T(8,128)S(1)} %get-tuple-element.9.which_ref, f32[4,128]{1,0:T(4,128)S(1)} %get-tuple-element.10.tail_ref, f32[3,8,8,128]{3,2,1,0:T(8,128)S(1)} %get-tuple-element.11.points_ref, s32[8,8,128]{2,1,0:T(8,128)S(1)} %get-tuple-element.12.lanes_ref, ...), custom_call_target="tpu_custom_call" | custom-call | tf_op jit(solution)/shard_map/moments/pallas_call | solution.py:518
  19.9 4.2 %all-to-all-start = ((f32[32,3,4,128]{3,2,1,0:T(4,128)}), f32[32,3,4,128]{3,2,1,0:T(4,128)S(1)}, u32[]{:S(2)}, u32[]{:S(2)}) async-start(f32[32,3,4,128]{3,2,1,0:T(4,128)} %moments.1), calls=%async_computation | async-start | bytes 393216 | tf_op jit(solution)/shard_map/all_to_all | solution.py:526
  24.1 0.0 copy-start.1
  24.1 9.2 %all-to-all-done.rows_ref = f32[32,3,4,128]{3,2,1,0:T(4,128)S(1)} async-done(((f32[32,3,4,128]{3,2,1,0:T(4,128)}), f32[32,3,4,128]{3,2,1,0:T(4,128)S(1)}, u32[]{:S(2)}, u32[]{:S(2)}) %all-to-all-start) | async-done | bytes 196640 | tf_op jit(solution)/shard_map/all_to_all | solution.py:526
  33.3 0.0 copy-done.1
  33.3 2.4 %solve.1 = f32[4,12]{1,0:T(4,128)} custom-call(s32[1]{0:T(128)} %bitcast.first_ref, f32[12,128]{1,0:T(8,128)S(1)} %copy-done.1, f32[32,3,4,128]{3,2,1,0:T(4,128)S(1)} %all-to-all-done.rows_ref), custom_call_target="tpu_custom_call" | custom-call | tf_op jit(solution)/shard_map/solve/pallas_call | solution.py:528
  (10 shorter events, 0.2 us)
Async XLA Ops:
  0.0 0.9 %copy-start = (f32[4,8,6,128]{3,1,2,0:T(8,128)S(1)}, f32[4,8,6,128]{3,1,2,0:T(8,128)}, u32[]{:S(2)}) copy-start(f32[4,8,6,128]{3,1,2,0:T(8,128)} %param.9) | copy-start | bytes 294916
  0.9 8.3 %collective-permute-start = (f32[32,4,128]{2,1,0:T(4,128)S(1)}, f32[32,4,128]{2,1,0:T(4,128)S(1)}, u32[]{:S(2)}, u32[]{:S(2)}) collective-permute-start(f32[32,4,128]{2,1,0:T(4,128)S(1)} %pack.1), channel_id=1, source_target_pairs={{28,0},{0,4},{4,8},{8,12},{12,16},{16,20},{20,24},{24,28},{29,1},{... | collective-permute-start | bytes 196616 | tf_op jit(solution)/shard_map/ppermute | solution.py:55
  3.0 6.2 %collective-permute-start.1 = (f32[32,4,128]{2,1,0:T(4,128)S(1)}, f32[32,4,128]{2,1,0:T(4,128)S(1)}, u32[]{:S(2)}, u32[]{:S(2)}) collective-permute-start(f32[32,4,128]{2,1,0:T(4,128)S(1)} %pack.1), channel_id=1, source_target_pairs={{4,0},{8,4},{12,8},{16,12},{20,16},{24,20},{28,24},{0,28},{5,1},{9... | collective-permute-start | bytes 196616 | tf_op jit(solution)/shard_map/ppermute | solution.py:56
  6.2 3.1 %collective-permute-start.2 = (f32[32,4,128]{2,1,0:T(4,128)S(1)}, f32[32,4,128]{2,1,0:T(4,128)S(1)}, u32[]{:S(2)}, u32[]{:S(2)}) collective-permute-start(f32[32,4,128]{2,1,0:T(4,128)S(1)} %pack.1), channel_id=1, source_target_pairs={{2,0},{3,1},{0,2},{1,3},{6,4},{7,5},{4,6},{5,7},{10,8},{11,9},{8,1... | collective-permute-start | bytes 196616 | tf_op jit(solution)/shard_map/ppermute | solution.py:62
  9.4 8.2 %collective-permute-start.3 = (f32[128,4,128]{2,1,0:T(4,128)S(1)}, f32[128,4,128]{2,1,0:T(4,128)S(1)}, u32[]{:S(2)}, u32[]{:S(2)}) collective-permute-start(f32[128,4,128]{2,1,0:T(4,128)S(1)} %pad_maximum_fusion), channel_id=1, source_target_pairs={{1,0},{0,1},{3,2},{2,3},{5,4},{4,5},{7,6},{6,7},{9,8},{8,9},{11,10... | collective-permute-start | bytes 786440 | tf_op jit(solution)/shard_map/ppermute | solution.py:62
  11.5 3.7 %collective-permute-start.4 = (f32[32,4,128]{2,1,0:T(4,128)S(1)}, f32[32,4,128]{2,1,0:T(4,128)S(1)}, u32[]{:S(2)}, u32[]{:S(2)}) collective-permute-start(f32[32,4,128]{2,1,0:T(4,128)S(1)} %collective-permute-done), channel_id=1, source_target_pairs={{2,0},{3,1},{0,2},{1,3},{6,4},{7,5},{4,6},{5,7},{10,8},{11,9},{8,1... | collective-permute-start | bytes 196616 | tf_op jit(solution)/shard_map/ppermute | solution.py:62
  12.9 3.5 %collective-permute-start.5 = (f32[32,4,128]{2,1,0:T(4,128)S(1)}, f32[32,4,128]{2,1,0:T(4,128)S(1)}, u32[]{:S(2)}, u32[]{:S(2)}) collective-permute-start(f32[32,4,128]{2,1,0:T(4,128)S(1)} %collective-permute-done.1), channel_id=1, source_target_pairs={{2,0},{3,1},{0,2},{1,3},{6,4},{7,5},{4,6},{5,7},{10,8},{11,9},{8,1... | collective-permute-start | bytes 196616 | tf_op jit(solution)/shard_map/ppermute | solution.py:62
  16.5 2.1 %collective-permute-start.6 = (f32[64,4,128]{2,1,0:T(4,128)S(1)}, f32[64,4,128]{2,1,0:T(4,128)S(1)}, u32[]{:S(2)}, u32[]{:S(2)}) collective-permute-start(f32[64,4,128]{2,1,0:T(4,128)S(1)} %pad_maximum_fusion.1), channel_id=1, source_target_pairs={{1,0},{0,1},{3,2},{2,3},{5,4},{4,5},{7,6},{6,7},{9,8},{8,9},{11,10... | collective-permute-start | bytes 393224 | tf_op jit(solution)/shard_map/ppermute | solution.py:62
  19.9 13.4 %all-to-all-start = ((f32[32,3,4,128]{3,2,1,0:T(4,128)}), f32[32,3,4,128]{3,2,1,0:T(4,128)S(1)}, u32[]{:S(2)}, u32[]{:S(2)}) async-start(f32[32,3,4,128]{3,2,1,0:T(4,128)} %moments.1), calls=%async_computation | async-start | bytes 393216 | tf_op jit(solution)/shard_map/all_to_all | solution.py:526
  24.1 9.2 %copy-start.1 = (f32[12,128]{1,0:T(8,128)S(1)}, f32[12,128]{1,0:T(8,128)}, u32[]{:S(2)}) copy-start(f32[12,128]{1,0:T(8,128)} %pose_ref.1) | copy-start | bytes 18436
